TPU v7x, 32 devices: a whole 2x2x4 slice. The times are simulated.
32 devices in a mesh: members: 2 (over y), band: 4 (over z), head: 4 (over x, core).
Axes of the slice: x: 2, y: 2, z: 4, core: 2. Of those that a mesh axis runs over, the one named last changes fastest.
Arguments:
- grid_feats: bfloat16 [4096, 1024], P(('members', 'band')), parts along dimension 0, may hold values from -6 to 6
- mesh_feats: bfloat16 [4096, 1024], P(('members', 'band')), parts along dimension 0, may hold values from -6 to 6
- enc_in: bfloat16 [3, 1024, 1024], P(None, 'band', 'head'), may hold values from -0.19921875 to 0.19921875
- enc_out: bfloat16 [1024, 1024], P('head', 'band'), may hold values from -0.1875 to 0.1875
- proc_in: bfloat16 [3, 1024, 1024], P(None, 'band', 'head'), may hold values from -0.19921875 to 0.19921875
- proc_out: bfloat16 [1024, 1024], P('head', 'band'), may hold values from -0.1875 to 0.1875
- ff_up: bfloat16 [1024, 4096], P('band', 'head'), may hold values from -0.1875 to 0.1875
- ff_down: bfloat16 [4096, 1024], P('head', 'band'), may hold values from -0.09375 to 0.09375
- dec_in: bfloat16 [3, 1024, 1024], P(None, 'band', 'head'), may hold values from -0.19921875 to 0.19921875
- dec_out: bfloat16 [1024, 1024], P('head', 'band'), may hold values from -0.1875 to 0.1875
- enc_list: int32 [16, 8], replicated, may hold values from 0 to 15, as said below
- enc_count: int32 [16], replicated, may hold values from 1 to 8
- dec_list: int32 [16, 8], replicated, may hold values from 0 to 15, as said below
- dec_count: int32 [16], replicated, may hold values from 1 to 8
- window_ids: int32 [2048], replicated, may hold values from 0 to 1, never falling along the last dimension, each value on 1 to 1536 neighbouring positions
Outputs:
- grid_out: bfloat16 [4096, 1024], P(('members', 'band', 'head')), parts along dimension 0
There are 2 independent parts, one for each index of `members`. A program takes and returns all parts, laid end to end along the dimension named above; an argument that names none is the same for every part. Nothing has to cross between parts.
Inputs may be any that keep to these rules, and one draw needn't show every extreme that they name: `enc_list`: each row holds distinct block numbers. Every block listed for mesh block m lies in the band of 512 grid points with the same band number as m's band of 512 nodes, or in the band just before or just after it. Only the first enc_count[m] slots of row m of enc_list are used. `dec_list`: each row holds distinct block numbers. Every block listed for grid block g lies in the band of 512 mesh nodes with the same band number as g's band of 512 grid points, or in the band just before or just after it. Only the first dec_count[g] slots of row g of dec_list are used. `window_ids`: never falls along the nodes; each window holds at most 1536 consecutive nodes.
All inputs are finite; a program needn't handle non-finite values.
Results may differ from a plain program's by a relative error of at most 0.02.
Values may be sent and summed in bfloat16 or wider, within the bound.
No kernel may reach another device: no remote copies, remote signals or barrier semaphores. Data moves between devices by JAX's collectives and lax.ppermute only.
A program may use at most 64 MiB of HBM per device.

v0:
```python
import functools

import jax
import jax.numpy as jnp
from jax import lax
from jax.experimental import pallas as pl
from jax.experimental.pallas import tpu as pltpu
from jax.sharding import PartitionSpec as P


HD = 64
BLOCK = 128
WINDOW = 1536
LANES = 128

EPSILON = 1e-05
NEGATIVE = -1e30


def dot(a, b):
    return jnp.dot(a, b, preferred_element_type=jnp.float32)


def normed(values):
    values = values.astype(jnp.float32)
    centred = values - jnp.mean(values, axis=-1, keepdims=True)
    variance = jnp.mean(centred * centred, axis=-1, keepdims=True)
    return (centred * lax.rsqrt(variance + EPSILON)).astype(jnp.bfloat16)


def exchange(value, axis, bit):
    count = lax.axis_size(axis)
    return lax.ppermute(value, axis, [(i, i ^ bit) for i in range(count)])


def half_shard(weight, members):
    rows = weight.shape[0] // members
    return lax.dynamic_slice_in_dim(weight, lax.axis_index("members") * rows, rows, 0)


def gather(value):
    members, bands = lax.axis_size("members"), lax.axis_size("band")
    whole = lax.all_gather(value, ("members", "band"), axis=0, tiled=False)
    return whole.reshape((members, bands) + value.shape)


def by_rows(pieces):
    members, bands, rows, columns = pieces.shape
    return pieces.transpose(1, 0, 2, 3).reshape(bands * members * rows, columns)


def by_columns(pieces):
    members, bands, rows, columns = pieces.shape
    return pieces.transpose(0, 2, 1, 3).reshape(members * rows, bands * columns)


def gather_projections(w_in, w_out):
    members = lax.axis_size("members")
    k_rows = w_in.shape[1] // members
    o_rows = w_out.shape[0] // members
    member = lax.axis_index("members")
    part_in = lax.dynamic_slice_in_dim(w_in, member * k_rows, k_rows, 1)
    part_out = half_shard(w_out, members)
    width = w_in.shape[2]
    flat_in = part_in.reshape(3 * k_rows, width)
    flat_out = part_out.reshape(-1, width)
    pieces = gather(jnp.concatenate([flat_in, flat_out], axis=0))
    bands = pieces.shape[1]
    mats = [by_rows(pieces[:, :, i * k_rows : (i + 1) * k_rows]) for i in range(3)]
    outs = pieces[:, :, 3 * k_rows :].reshape(members, bands, o_rows, w_out.shape[1])
    return mats, by_columns(outs)


def attention_kernel(pieces, keyed, *refs):
    q_ref = refs[0]
    kv_refs = refs[1 : 1 + pieces]
    mask_refs = refs[1 + pieces : -1]
    out_ref = refs[-1]
    width = q_ref.shape[1]
    rows = q_ref.shape[0]
    sizes = [ref.shape[1] for ref in kv_refs]
    if keyed:
        ids = mask_refs[0][...]
        biases = [
            jnp.where(ids == mask_refs[1][i], 0.0, NEGATIVE).astype(jnp.float32)
            for i in range(pieces)
        ]
    else:
        biases = [mask_refs[0][0, i] for i in range(pieces)]
    lane = lax.broadcasted_iota(jnp.int32, (rows, LANES), 1)
    for pair in range(width // LANES):
        cols = slice(pair * LANES, (pair + 1) * LANES)
        queries = q_ref[:, cols]
        halves = []
        for odd in range(LANES // HD):
            mine = (lane >= odd * HD) & (lane < (odd + 1) * HD)
            picked = jnp.where(mine, queries.astype(jnp.float32) * HD ** (-0.5), 0.0).astype(
                jnp.bfloat16
            )
            scores = [
                lax.dot_general(
                    picked,
                    kv_refs[i][0, :, cols],
                    (((1,), (1,)), ((), ())),
                    preferred_element_type=jnp.float32,
                )
                + biases[i]
                for i in range(pieces)
            ]
            top = functools.reduce(
                jnp.maximum, [jnp.max(part, axis=1, keepdims=True) for part in scores]
            )
            total = None
            for i in range(pieces):
                weights = jnp.exp(scores[i] - top).astype(jnp.bfloat16)
                values = jnp.concatenate(
                    [kv_refs[i][1, :, cols], jnp.ones((sizes[i], LANES), jnp.bfloat16)], axis=1
                )
                part = dot(weights, values)
                total = part if total is None else total + part
            halves.append((mine, total[:, :LANES] / total[:, LANES:]))
        merged = halves[0][1]
        for mine, half in halves[1:]:
            merged = jnp.where(mine, half, merged)
        out_ref[:, cols] = merged.astype(jnp.bfloat16)


def attend(queries, kv_list, masks, keyed):
    rows, width = queries.shape
    pieces = len(kv_list)
    whole = lambda value: pl.BlockSpec(value.shape, lambda i: (0,) * value.ndim)
    if keyed:
        mask_specs = [pl.BlockSpec((BLOCK, 1), lambda i: (i, 0)), whole(masks[1])]
    else:
        mask_specs = [pl.BlockSpec((1,) + masks[0].shape[1:], lambda i: (i, 0, 0, 0))]
    return pl.pallas_call(
        functools.partial(attention_kernel, pieces, keyed),
        grid=(rows // BLOCK,),
        in_specs=[pl.BlockSpec((BLOCK, width), lambda i: (i, 0))]
        + [whole(kv) for kv in kv_list]
        + mask_specs,
        out_specs=pl.BlockSpec((BLOCK, width), lambda i: (i, 0)),
        out_shape=jax.ShapeDtypeStruct((rows, width), jnp.bfloat16),
        compiler_params=pltpu.CompilerParams(dimension_semantics=("arbitrary",)),
    )(queries, *kv_list, *masks)


def list_bias(lists, counts, band_index, query_blocks, pool_blocks):
    mine = lax.dynamic_slice_in_dim(lists, band_index * query_blocks, query_blocks, 0)
    used = lax.dynamic_slice_in_dim(counts, band_index * query_blocks, query_blocks, 0)
    live = jnp.arange(lists.shape[1], dtype=jnp.int32)[None, :] < used[:, None]
    candidates = (band_index - 1) * pool_blocks + jnp.arange(3 * pool_blocks, dtype=jnp.int32)
    hit = (mine[:, :, None] == candidates[None, None, :]) & live[:, :, None]
    bias = jnp.where(jnp.any(hit, axis=1), 0.0, NEGATIVE).astype(jnp.float32)
    spread = jnp.broadcast_to(bias[:, :, None], bias.shape + (BLOCK,))
    return spread.reshape(query_blocks, 3, 1, pool_blocks * BLOCK)


def neighbours(block):
    count = lax.axis_size("band")
    forward = [(i, i + 1) for i in range(count - 1)]
    backward = [(target, source) for source, target in forward]
    return lax.ppermute(block, "band", forward), lax.ppermute(block, "band", backward)


def half_of(value, index):
    rows = value.shape[0] // 2
    return lax.dynamic_slice_in_dim(value, index * rows, rows, 0)


def head_sum_half(source, weight, side):
    away = dot(half_of(source, 1 - side), weight).astype(jnp.bfloat16)
    came = exchange(away, "head", 1)
    total = dot(half_of(source, side), weight).astype(jnp.bfloat16).astype(jnp.float32)
    total = total + came.astype(jnp.float32)
    bit = 2
    while bit < lax.axis_size("head"):
        sent = total.astype(jnp.bfloat16)
        total = sent.astype(jnp.float32) + exchange(sent, "head", bit).astype(jnp.float32)
        bit *= 2
    return total


def both_halves(half, side):
    other = exchange(half, "head", 1)
    low = jnp.where(side == 0, half, other)
    high = jnp.where(side == 0, other, half)
    return jnp.concatenate([low, high], axis=0)


def per_device(
    grid_feats,
    mesh_feats,
    enc_in,
    enc_out,
    proc_in,
    proc_out,
    ff_up,
    ff_down,
    dec_in,
    dec_out,
    enc_list,
    enc_count,
    dec_list,
    dec_count,
    window_ids,
):
    members = lax.axis_size("members")
    bands = lax.axis_size("band")
    heads = lax.axis_size("head")
    band_index = lax.axis_index("band")
    head_index = lax.axis_index("head")
    side = head_index % 2
    grid_rows = grid_feats.shape[0]
    mesh_rows = mesh_feats.shape[0]
    grid_blocks = grid_rows // BLOCK
    mesh_blocks = mesh_rows // BLOCK

    enc_w, enc_o = gather_projections(enc_in, enc_out)
    proc_w, proc_o = gather_projections(proc_in, proc_out)
    up = by_rows(gather(half_shard(ff_up, members)))
    down = by_columns(gather(half_shard(ff_down, members)))
    dec_w, dec_o = gather_projections(dec_in, dec_out)

    enc_bias = list_bias(enc_list, enc_count, band_index, mesh_blocks, grid_blocks)
    dec_bias = list_bias(dec_list, dec_count, band_index, grid_blocks, mesh_blocks)

    grid_norm = normed(grid_feats)
    mesh_norm = normed(mesh_feats)

    def project(source, weight):
        return dot(source, weight).astype(jnp.bfloat16)

    enc_kv = jnp.stack([project(grid_norm, enc_w[1]), project(grid_norm, enc_w[2])])
    low, high = neighbours(enc_kv)
    enc_q = project(mesh_norm, enc_w[0])
    enc_attn = attend(enc_q, [low, enc_kv, high], [enc_bias], False)
    state = half_of(mesh_feats, side).astype(jnp.float32) + head_sum_half(enc_attn, enc_o, side)

    proc_norm = both_halves(normed(state), side)
    pairs = jnp.stack([project(proc_norm, proc_w[1]), project(proc_norm, proc_w[2])])
    reach = (WINDOW + mesh_rows - 2) // mesh_rows
    if bands <= 2 * reach + 1:
        offsets = list(range(1, bands))
        routes = [[(i, (i - offset) % bands) for i in range(bands)] for offset in offsets]
    else:
        offsets = [sign * step for step in range(1, reach + 1) for sign in (1, -1)]
        routes = [
            [(i, i - offset) for i in range(bands) if 0 <= i - offset < bands]
            for offset in offsets
        ]
    slab = [pairs] + [lax.ppermute(pairs, "band", route) for route in routes]
    key_ids = []
    for offset in [0] + offsets:
        source = band_index + offset
        if bands <= 2 * reach + 1:
            source = source % bands
        inside = (source >= 0) & (source < bands)
        safe = jnp.clip(source, 0, bands - 1)
        ids = lax.dynamic_slice_in_dim(window_ids, safe * mesh_rows, mesh_rows, 0)
        key_ids.append(jnp.where(inside, ids, -1).reshape(1, mesh_rows))
    key_ids = jnp.stack(key_ids)
    query_ids = lax.dynamic_slice_in_dim(
        window_ids, band_index * mesh_rows, mesh_rows, 0
    ).reshape(mesh_rows, 1)
    proc_q = project(proc_norm, proc_w[0])
    proc_attn = attend(proc_q, slab, [query_ids, key_ids], True)
    state = state + head_sum_half(proc_attn, proc_o, side)

    ff_norm = both_halves(normed(state), side)
    hidden = jax.nn.gelu(dot(ff_norm, up), approximate=False).astype(jnp.bfloat16)
    state = state + head_sum_half(hidden, down, side)

    final_norm = both_halves(normed(state), side)
    dec_kv = jnp.stack([project(final_norm, dec_w[1]), project(final_norm, dec_w[2])])
    low, high = neighbours(dec_kv)
    dec_q = project(grid_norm, dec_w[0])
    dec_attn = attend(dec_q, [low, dec_kv, high], [dec_bias], False)

    share = grid_rows // heads
    rows_of = dec_attn.reshape(heads // 2, 2, share, dec_attn.shape[1])

    def side_product(which):
        picked = lax.dynamic_index_in_dim(rows_of, which, 1, keepdims=False)
        return dot(picked.reshape(-1, picked.shape[-1]), dec_o).astype(jnp.bfloat16)

    came = exchange(side_product(1 - side), "head", 1)
    total = side_product(side).astype(jnp.float32) + came.astype(jnp.float32)
    bit = 2
    position = head_index // 2
    while bit < heads:
        parts = total.reshape(-1, 2, share, total.shape[1])
        mine = position % 2
        send = lax.dynamic_index_in_dim(parts, 1 - mine, 1, keepdims=False)
        keep = lax.dynamic_index_in_dim(parts, mine, 1, keepdims=False)
        got = exchange(send.astype(jnp.bfloat16), "head", bit)
        total = (
            keep.astype(jnp.bfloat16).astype(jnp.float32) + got.astype(jnp.float32)
        ).reshape(-1, total.shape[1])
        position = position // 2
        bit *= 2
    residual = lax.dynamic_slice_in_dim(grid_feats, head_index * share, share, 0)
    return (residual.astype(jnp.float32) + total).astype(jnp.bfloat16)


def own_half(weight, axis):
    size = weight.shape[axis] // 2
    return lax.dynamic_slice_in_dim(weight, lax.axis_index("members") * size, size, axis)


def swap(value):
    return lax.ppermute(value, "members", [(0, 1), (1, 0)])


def stacked_columns(weight):
    return jnp.concatenate(
        [weight[:, i : i + LANES] for i in range(0, weight.shape[1], LANES)], axis=0
    )


def pack(w_in, w_out, which):
    parts = {name: own_half(w_in[i], 1) for i, name in enumerate("qkv") if name in which}
    if "o" in which:
        parts["o"] = stacked_columns(own_half(w_out, 0))
    return jnp.concatenate([parts[name] for name in which], axis=1)


def band_gather(value):
    return lax.all_gather(value, "band", axis=0, tiled=True)


def project_kernel(widths, *refs):
    source, own, other = refs[:3]
    for (start, width), out in zip(widths, refs[3:]):
        for place, weight in enumerate((own, other)):
            out[:, place * width : (place + 1) * width] = dot(
                source[...], weight[:, start : start + width]
            ).astype(jnp.bfloat16)


def project_pair(source, own, other, widths):
    rows = source.shape[0]
    return pl.pallas_call(
        functools.partial(project_kernel, widths),
        out_shape=[jax.ShapeDtypeStruct((rows, 2 * w), jnp.bfloat16) for _, w in widths],
    )(source, own, other)


def pair_attention_kernel(pieces, keyed, o_start, order_ref, *refs):
    q_ref = refs[0]
    kv_refs = refs[1 : 1 + pieces]
    masks = 2 if keyed else 1
    mask_refs = refs[1 + pieces : 1 + pieces + masks]
    weight_refs = refs[1 + pieces + masks : 3 + pieces + masks]
    away_ref, keep_ref = refs[3 + pieces + masks :]
    rows = q_ref.shape[0]
    step = pl.program_id(0)
    half = pl.num_programs(0) // 2
    if keyed:
        ids = mask_refs[0][...]
        biases = [
            jnp.where(ids == mask_refs[1][i], 0.0, NEGATIVE).astype(jnp.float32)
            for i in range(pieces)
        ]
    else:
        biases = [mask_refs[0][0, i] for i in range(pieces)]
    lane = lax.broadcasted_iota(jnp.int32, (rows, LANES), 1)
    mixed = []
    for pair in range(2):
        queries = q_ref[:, pair * LANES : (pair + 1) * LANES]
        key_cols = slice(2 * pair * LANES, (2 * pair + 1) * LANES)
        value_cols = slice((2 * pair + 1) * LANES, (2 * pair + 2) * LANES)
        merged = None
        for odd in range(LANES // HD):
            mine = (lane >= odd * HD) & (lane < (odd + 1) * HD)
            picked = jnp.where(mine, queries.astype(jnp.float32) * HD ** (-0.5), 0.0).astype(
                jnp.bfloat16
            )
            scores = [
                lax.dot_general(
                    picked,
                    kv_refs[i][:, key_cols],
                    (((1,), (1,)), ((), ())),
                    preferred_element_type=jnp.float32,
                )
                + biases[i]
                for i in range(pieces)
            ]
            top = functools.reduce(
                jnp.maximum, [jnp.max(part, axis=1, keepdims=True) for part in scores]
            )
            total = None
            for i in range(pieces):
                weights = jnp.exp(scores[i] - top).astype(jnp.bfloat16)
                values = kv_refs[i][:, value_cols]
                values = jnp.concatenate([values, jnp.ones_like(values)], axis=1)
                part = dot(weights, values)
                total = part if total is None else total + part
            result = total[:, :LANES] / total[:, LANES:]
            merged = result if merged is None else jnp.where(mine, result, merged)
        mixed.append(merged.astype(jnp.bfloat16))

    def write(out_ref):
        for group in range(out_ref.shape[1] // LANES):
            cols = slice(group * LANES, (group + 1) * LANES)
            total = None
            for pair in range(2):
                part = dot(mixed[pair], weight_refs[pair][cols, o_start : o_start + LANES])
                total = part if total is None else total + part
            out_ref[:, cols] = total.astype(jnp.bfloat16)

    @pl.when(step < half)
    def _():
        write(away_ref)

    @pl.when(step >= half)
    def _():
        write(keep_ref)


def attend_pair(queries, kv_list, masks, keyed, weights, o_start, order):
    rows = queries.shape[0]
    blocks = rows // BLOCK
    features = weights[0].shape[0]
    pieces = len(kv_list)
    whole = lambda value: pl.BlockSpec(value.shape, lambda i, o: (0,) * value.ndim)
    if keyed:
        mask_specs = [pl.BlockSpec((BLOCK, 1), lambda i, o: (o[i], 0)), whole(masks[1])]
    else:
        mask_specs = [pl.BlockSpec((1,) + masks[0].shape[1:], lambda i, o: (o[i], 0, 0, 0))]
    half = blocks // 2
    out = jax.ShapeDtypeStruct((rows // 2, features), jnp.bfloat16)
    return pl.pallas_call(
        functools.partial(pair_attention_kernel, pieces, keyed, o_start),
        grid_spec=pltpu.PrefetchScalarGridSpec(
            num_scalar_prefetch=1,
            grid=(blocks,),
            in_specs=[pl.BlockSpec((BLOCK, queries.shape[1]), lambda i, o: (o[i], 0))]
            + [whole(kv) for kv in kv_list]
            + mask_specs
            + [whole(weight) for weight in weights],
            out_specs=[
                pl.BlockSpec((BLOCK, features), lambda i, o: (jnp.minimum(i, half - 1), 0)),
                pl.BlockSpec((BLOCK, features), lambda i, o: (jnp.maximum(i - half, 0), 0)),
            ],
        ),
        out_shape=[out, out],
        compiler_params=pltpu.CompilerParams(dimension_semantics=("arbitrary",)),
    )(order, queries, *kv_list, *masks, *weights)


def down_kernel(bands, order_ref, own_hidden, other_hidden, own, other, away_ref, keep_ref):
    step = pl.program_id(0)
    columns = own.shape[1]
    inner = own_hidden.shape[1]

    def write(out_ref):
        for band in range(bands):
            rows = slice(band * inner, (band + 1) * inner)
            out_ref[:, band * columns : (band + 1) * columns] = (
                dot(own_hidden[...], own[rows, :]) + dot(other_hidden[...], other[rows, :])
            ).astype(jnp.bfloat16)

    @pl.when(step == 0)
    def _():
        write(away_ref)

    @pl.when(step == 1)
    def _():
        write(keep_ref)


def down_pair(own_hidden, other_hidden, own, other, order):
    rows, inner = own_hidden.shape
    bands = own.shape[0] // inner
    features = bands * own.shape[1]
    whole = lambda value: pl.BlockSpec(value.shape, lambda i, o: (0,) * value.ndim)
    taken = pl.BlockSpec((rows // 2, inner), lambda i, o: (o[i], 0))
    placed = pl.BlockSpec((rows // 2, features), lambda i, o: (0, 0))
    out = jax.ShapeDtypeStruct((rows // 2, features), jnp.bfloat16)
    return pl.pallas_call(
        functools.partial(down_kernel, bands),
        grid_spec=pltpu.PrefetchScalarGridSpec(
            num_scalar_prefetch=1,
            grid=(2,),
            in_specs=[taken, taken, whole(own), whole(other)],
            out_specs=[placed, placed],
        ),
        out_shape=[out, out],
        compiler_params=pltpu.CompilerParams(dimension_semantics=("arbitrary",)),
    )(order, own_hidden, other_hidden, own, other)


def sum_over_head(away, keep):
    total = keep.astype(jnp.float32) + exchange(away, "head", 1).astype(jnp.float32)
    bit = 2
    while bit < lax.axis_size("head"):
        sent = total.astype(jnp.bfloat16)
        total = sent.astype(jnp.float32) + exchange(sent, "head", bit).astype(jnp.float32)
        bit *= 2
    return total


def slab_routes(bands, mesh_rows):
    reach = (WINDOW + mesh_rows - 2) // mesh_rows
    if bands <= 2 * reach + 1:
        offsets = list(range(1, bands))
        return True, offsets, [[(i, (i - o) % bands) for i in range(bands)] for o in offsets]
    offsets = [sign * step for step in range(1, reach + 1) for sign in (1, -1)]
    routes = [[(i, i - o) for i in range(bands) if 0 <= i - o < bands] for o in offsets]
    return False, offsets, routes


def slab_ids(window_ids, mesh_rows, offsets, around):
    bands = lax.axis_size("band")
    key_ids = []
    for offset in [0] + offsets:
        source = lax.axis_index("band") + offset
        if around:
            source = source % bands
        inside = (source >= 0) & (source < bands)
        safe = jnp.clip(source, 0, bands - 1)
        ids = lax.dynamic_slice_in_dim(window_ids, safe * mesh_rows, mesh_rows, 0)
        key_ids.append(jnp.where(inside, ids, -1).reshape(1, mesh_rows))
    query_ids = lax.dynamic_slice_in_dim(
        window_ids, lax.axis_index("band") * mesh_rows, mesh_rows, 0
    ).reshape(mesh_rows, 1)
    return query_ids, jnp.stack(key_ids)


def paired_device(
    grid_feats,
    mesh_feats,
    enc_in,
    enc_out,
    proc_in,
    proc_out,
    ff_up,
    ff_down,
    dec_in,
    dec_out,
    enc_list,
    enc_count,
    dec_list,
    dec_count,
    window_ids,
):
    bands = lax.axis_size("band")
    heads = lax.axis_size("head")
    band_index = lax.axis_index("band")
    head_index = lax.axis_index("head")
    side = head_index % 2
    grid_rows = grid_feats.shape[0]
    mesh_rows = mesh_feats.shape[0]
    grid_blocks = grid_rows // BLOCK
    mesh_blocks = mesh_rows // BLOCK
    half_blocks = mesh_blocks // 2
    turns = jnp.arange(mesh_blocks, dtype=jnp.int32)
    order = (turns + (1 - side) * half_blocks) % mesh_blocks
    sides = jnp.stack([1 - side, side]).astype(jnp.int32)
    barrier = lax.optimization_barrier
    kv_cols, q_cols = (0, 2 * LANES), (2 * LANES, LANES)
    o_start = 3 * LANES

    enc_kv_own = band_gather(pack(enc_in, enc_out, "kv"))
    enc_kv_other = swap(enc_kv_own)
    enc_qo_own = band_gather(barrier((pack(enc_in, enc_out, "qo"), enc_kv_own))[0])
    enc_qo_other = swap(enc_qo_own)
    packed = (
        pack(proc_in, proc_out, "kvqo"),
        own_half(ff_up, 1),
        own_half(ff_down, 0),
        pack(dec_in, dec_out, "kvqo"),
    )
    packed = barrier(packed + (enc_kv_own,))[:4]
    proc_own, up_own, down_own, dec_own = [band_gather(value) for value in packed]
    proc_other = swap(proc_own)
    up_other = swap(up_own)
    down_other = swap(down_own)
    dec_other = swap(dec_own)

    enc_bias = list_bias(enc_list, enc_count, band_index, mesh_blocks, grid_blocks)
    dec_bias = list_bias(dec_list, dec_count, band_index, grid_blocks, mesh_blocks)
    around, offsets, routes = slab_routes(bands, mesh_rows)
    query_ids, key_ids = slab_ids(window_ids, mesh_rows, offsets, around)

    grid_norm = normed(grid_feats)
    mesh_norm = normed(mesh_feats)

    (enc_kv,) = project_pair(grid_norm, enc_kv_own, enc_kv_other, [kv_cols])
    low, high = neighbours(enc_kv)
    (enc_q,) = project_pair(mesh_norm, enc_qo_own, enc_qo_other, [(0, LANES)])
    away, keep = attend_pair(
        enc_q, [low, enc_kv, high], [enc_bias], False, [enc_qo_own, enc_qo_other], LANES, order
    )
    state = half_of(mesh_feats, side).astype(jnp.float32) + sum_over_head(away, keep)

    proc_norm = both_halves(normed(state), side)
    proc_kv, proc_q = project_pair(proc_norm, proc_own, proc_other, [kv_cols, q_cols])
    slab = [proc_kv] + [lax.ppermute(proc_kv, "band", route) for route in routes]
    away, keep = attend_pair(
        proc_q, slab, [query_ids, key_ids], True, [proc_own, proc_other], o_start, order
    )
    state = state + sum_over_head(away, keep)

    ff_norm = both_halves(normed(state), side)
    hidden = [
        jax.nn.gelu(dot(ff_norm, up), approximate=False).astype(jnp.bfloat16)
        for up in (up_own, up_other)
    ]
    away, keep = down_pair(*hidden, down_own, down_other, sides)
    state = state + sum_over_head(away, keep)

    final_norm = both_halves(normed(state), side)
    (dec_q,) = project_pair(grid_norm, dec_own, dec_other, [q_cols])
    (dec_kv,) = project_pair(final_norm, dec_own, dec_other, [kv_cols])
    low, high = neighbours(dec_kv)
    share = grid_rows // heads
    by_core = turns.reshape(-1, 2, share // BLOCK).transpose(1, 0, 2).reshape(2, -1)
    dec_order = jnp.where(side == 0, by_core[::-1].reshape(-1), by_core.reshape(-1))
    away, keep = attend_pair(
        dec_q, [low, dec_kv, high], [dec_bias], False, [dec_own, dec_other], o_start, dec_order
    )
    total = keep.astype(jnp.float32) + exchange(away, "head", 1).astype(jnp.float32)
    bit = 2
    position = head_index // 2
    while bit < heads:
        parts = total.reshape(-1, 2, share, total.shape[1])
        mine = position % 2
        send = lax.dynamic_index_in_dim(parts, 1 - mine, 1, keepdims=False)
        kept = lax.dynamic_index_in_dim(parts, mine, 1, keepdims=False)
        got = exchange(send.astype(jnp.bfloat16), "head", bit)
        total = (
            kept.astype(jnp.bfloat16).astype(jnp.float32) + got.astype(jnp.float32)
        ).reshape(-1, total.shape[1])
        position = position // 2
        bit *= 2
    residual = lax.dynamic_slice_in_dim(grid_feats, head_index * share, share, 0)
    return (residual.astype(jnp.float32) + total).astype(jnp.bfloat16)


def body(*args):
    w_in, w_out = args[2], args[3]
    paired = (
        lax.axis_size("members") == 2
        and w_in.shape[2] == 4 * HD
        and 2 * HD == LANES
        and w_in.shape[1] == w_out.shape[1]
        and w_in.shape[1] % LANES == 0
        and args[0].shape[0] % (lax.axis_size("head") * BLOCK) == 0
        and args[0].shape[0] == args[1].shape[0]
    )
    if not paired:
        return per_device(*args)
    return paired_device(*args)


def solution(mesh):
    return jax.shard_map(
        body,
        mesh=mesh,
        in_specs=(
            P(("members", "band"), None),
            P(("members", "band"), None),
            P(None, "band", "head"),
            P("head", "band"),
            P(None, "band", "head"),
            P("head", "band"),
            P("band", "head"),
            P("head", "band"),
            P(None, "band", "head"),
            P("head", "band"),
            P(),
            P(),
            P(),
            P(),
            P(),
        ),
        out_specs=P(("members", "band", "head"), None),
        check_vma=False,
    )
```

profile of v0, /device:TPU:0, one launch (start us, length us, event | category | flops | bytes accessed | tf_op | source)
XLA Modules:
  0.0 362.7 jit_solution(10178433965926745995)
XLA Ops:
  7.7 18.1 %all_gather.18.refs_1_ = bf16[1024,256]{1,0:T(8,128)(2,1)} all-gather(bf16[256,256]{1,0:T(8,128)(2,1)S(1)} %pad_maximum_fusion.9), channel_id=1, replica_groups=mesh['members'=2,'band'=4,'head'=4] {'band'}, dimensions={0}, use_global_device_ids=true | all-gather | bytes 655360 | tf_op jit(solution)/shard_map/all_gather | solution.py:329
  27.5 16.3 %all_gather.20.refs_1_.refs_5_ = bf16[1024,256]{1,0:T(8,128)(2,1)S(1)} all-gather(bf16[256,256]{1,0:T(8,128)(2,1)S(1)} %maximum_maximum_fusion.2), channel_id=1, replica_groups=mesh['members'=2,'band'=4,'head'=4] {'band'}, dimensions={0}, use_global_device_ids=true | all-gather | bytes 655360 | tf_op jit(solution)/shard_map/all_gather | solution.py:329
  53.9 3.7 %collective-permute-start.3 = (bf16[512,512]{1,0:T(8,128)(2,1)}, bf16[512,512]{1,0:T(8,128)(2,1)S(1)}, u32[]{:S(2)}, u32[]{:S(2)}) collective-permute-start(bf16[512,512]{1,0:T(8,128)(2,1)} %shard_map.147.refs_2_), channel_id=1, source_target_pairs={{0,4},{4,8},{8,12},{1,5},{5,9},{9,13},{2,6},{6,10},{10,14},{3,7},{... | collective-permute-start | bytes 1572872 | tf_op jit(solution)/shard_map/ppermute | solution.py:163
  64.5 11.5 %collective-permute-done.3.refs_1_ = bf16[512,512]{1,0:T(8,128)(2,1)S(1)} collective-permute-done((bf16[512,512]{1,0:T(8,128)(2,1)}, bf16[512,512]{1,0:T(8,128)(2,1)S(1)}, u32[]{:S(2)}, u32[]{:S(2)}) %collective-permute-start.3) | collective-permute-done | bytes 524320 | tf_op jit(solution)/shard_map/ppermute | solution.py:163
  75.9 7.7 %collective-permute-done.4.refs_3_ = bf16[512,512]{1,0:T(8,128)(2,1)S(1)} collective-permute-done((bf16[512,512]{1,0:T(8,128)(2,1)}, bf16[512,512]{1,0:T(8,128)(2,1)S(1)}, u32[]{:S(2)}, u32[]{:S(2)}) %collective-permute-start.4) | collective-permute-done | bytes 524320 | tf_op jit(solution)/shard_map/ppermute | solution.py:163
  84.4 10.2 %shard_map.148 = (bf16[256,1024]{1,0:T(8,128)(2,1)}, bf16[256,1024]{1,0:T(8,128)(2,1)}) custom-call(s32[4]{0:T(128)} %and_select_fusion.order_ref, bf16[512,256]{1,0:T(8,128)(2,1)} %shard_map.146.refs_0_, bf16[512,512]{1,0:T(8,128)(2,1)} %copy-done.12, bf16[512,512]{1,0:T(8,128)(2,1)} %shard_map.147.refs_2_, bf16[512,512]{1,0:T(8,128)(2,1)} %copy-done.13, ...), custom_call_target="tpu_custom_call" | custom-call | tf_op jit(solution)/shard_map/pallas_call | solution.py:433
  100.9 11.1 %collective-permute-done.6 = bf16[256,1024]{1,0:T(8,128)(2,1)S(1)} collective-permute-done((bf16[256,1024]{1,0:T(8,128)(2,1)S(1)}, bf16[256,1024]{1,0:T(8,128)(2,1)S(1)}, u32[]{:S(2)}, u32[]{:S(2)}) %collective-permute-start.6) | collective-permute-done | bytes 524320 | tf_op jit(solution)/shard_map/ppermute | solution.py:33
  117.3 7.4 %collective-permute-done.8.refs_2_.refs_8_ = bf16[1024,512]{1,0:T(8,128)(2,1)} collective-permute-done((bf16[1024,512]{1,0:T(8,128)(2,1)}, bf16[1024,512]{1,0:T(8,128)(2,1)}, u32[]{:S(2)}, u32[]{:S(2)}) %collective-permute-start.8) | collective-permute-done | bytes 1048608 | tf_op jit(solution)/shard_map/ppermute | solution.py:312
  124.7 3.8 %shard_map.149 = (bf16[512,512]{1,0:T(8,128)(2,1)}, bf16[512,256]{1,0:T(8,128)(2,1)}) custom-call(bf16[512,1024]{1,0:T(8,128)(2,1)} %pad_maximum_fusion.refs_0_, bf16[1024,512]{1,0:T(8,128)(2,1)} %all-gather.7.cloned.1.call-done.refs_1_.refs_7_, bf16[1024,512]{1,0:T(8,128)(2,1)} %collective-permute-done.8.refs_2_.refs_8_), custom_call_target="tpu_custom_call" | custom-call | tf_op jit(solution)/shard_map/pallas_call | solution.py:343
  134.4 47.6 %collective-permute-done.10.refs_3_ = bf16[512,512]{1,0:T(8,128)(2,1)S(1)} collective-permute-done((bf16[512,512]{1,0:T(8,128)(2,1)}, bf16[512,512]{1,0:T(8,128)(2,1)S(1)}, u32[]{:S(2)}, u32[]{:S(2)}) %collective-permute-start.10) | collective-permute-done | bytes 524320 | tf_op jit(solution)/shard_map/ppermute | solution.py:600
  183.0 12.3 %shard_map.150 = (bf16[256,1024]{1,0:T(8,128)(2,1)}, bf16[256,1024]{1,0:T(8,128)(2,1)}) custom-call(s32[4]{0:T(128)} %and_select_fusion.order_ref, bf16[512,256]{1,0:T(8,128)(2,1)} %get-tuple-element.25.refs_0_, bf16[512,512]{1,0:T(8,128)(2,1)} %get-tuple-element.26.refs_1_, bf16[512,512]{1,0:T(8,128)(2,1)} %collective-permute-done.9.refs_2_, ...), custom_call_target="tpu_custom_call" | custom-call | tf_op jit(solution)/shard_map/pallas_call | solution.py:433
  199.5 13.3 %collective-permute-done.13 = bf16[256,1024]{1,0:T(8,128)(2,1)} collective-permute-done((bf16[256,1024]{1,0:T(8,128)(2,1)S(1)}, bf16[256,1024]{1,0:T(8,128)(2,1)}, u32[]{:S(2)}, u32[]{:S(2)}) %collective-permute-start.13) | collective-permute-done | bytes 524320 | tf_op jit(solution)/shard_map/ppermute | solution.py:33
  218.0 18.1 %all-gather.11.cloned.1.call-done.own = bf16[2048,256]{1,0:T(8,128)(2,1)} async-done(((bf16[512,256]{1,0:T(8,128)(2,1)}), bf16[2048,256]{1,0:T(8,128)(2,1)}) %all-gather.11.cloned.1.call-update) | async-done | bytes 1048592 | tf_op jit(solution)/shard_map/all_gather | solution.py:329
  237.9 4.2 %fusion.10.own_hidden = bf16[512,512]{1,0:T(8,128)(2,1)} fusion(bf16[1024,512]{1,0:T(8,128)(2,1)S(1)} %copy-done.23, bf16[256,1024]{1,0:T(8,128)(2,1)S(1)} %get-tuple-element.42, bf16[256,1024]{1,0:T(8,128)(2,1)S(1)} %get-tuple-element.41), kind=kOutput, calls=%fused_computation.16 | convolution fusion | flops 556007424 | bytes 2621440 | tf_op jit(solution)/shard_map/dot_general | solution.py:21
  242.8 5.4 %fusion.13.other_hidden = bf16[512,512]{1,0:T(8,128)(2,1)} fusion(bf16[1024,512]{1,0:T(8,128)(2,1)} %collective-permute-done.15, bf16[256,1024]{1,0:T(8,128)(2,1)S(1)} %get-tuple-element.42, bf16[256,1024]{1,0:T(8,128)(2,1)S(1)} %get-tuple-element.41), kind=kOutput, calls=%fused_computation.19 | convolution fusion | flops 556007424 | bytes 2621440 | tf_op jit(solution)/shard_map/dot_general | solution.py:21
  248.2 16.5 %collective-permute-done.16.other = bf16[2048,256]{1,0:T(8,128)(2,1)S(1)} collective-permute-done((bf16[2048,256]{1,0:T(8,128)(2,1)}, bf16[2048,256]{1,0:T(8,128)(2,1)S(1)}, u32[]{:S(2)}, u32[]{:S(2)}) %collective-permute-start.16) | collective-permute-done | bytes 1048608 | tf_op jit(solution)/shard_map/ppermute | solution.py:312
  265.7 4.9 %shard_map.151 = (bf16[256,1024]{1,0:T(8,128)(2,1)}, bf16[256,1024]{1,0:T(8,128)(2,1)}) custom-call(s32[2]{0:T(128)} %pad_add_fusion.1.order_ref, bf16[512,512]{1,0:T(8,128)(2,1)} %fusion.10.own_hidden, bf16[512,512]{1,0:T(8,128)(2,1)} %fusion.13.other_hidden, bf16[2048,256]{1,0:T(8,128)(2,1)} %all-gather.11.cloned.1.call-done.own, bf16[2048,256]{1,0:T(8,128)(2,1)} %copy-done.7), custom_call_target="tpu_custom_call" | custom-call | tf_op jit(solution)/shard_map/pallas_call | solution.py:481
  276.0 12.0 %collective-permute-done.18 = bf16[256,1024]{1,0:T(8,128)(2,1)} collective-permute-done((bf16[256,1024]{1,0:T(8,128)(2,1)S(1)}, bf16[256,1024]{1,0:T(8,128)(2,1)}, u32[]{:S(2)}, u32[]{:S(2)}) %collective-permute-start.18) | collective-permute-done | bytes 524320 | tf_op jit(solution)/shard_map/ppermute | solution.py:33
  295.1 4.5 %collective-permute-done.refs_2_.refs_6_ = bf16[1024,512]{1,0:T(8,128)(2,1)S(1)} collective-permute-done((bf16[1024,512]{1,0:T(8,128)(2,1)}, bf16[1024,512]{1,0:T(8,128)(2,1)S(1)}, u32[]{:S(2)}, u32[]{:S(2)}) %collective-permute-start) | collective-permute-done | bytes 1048608 | tf_op jit(solution)/shard_map/ppermute | solution.py:312
  304.0 12.7 %collective-permute-start.20 = (bf16[512,512]{1,0:T(8,128)(2,1)}, bf16[512,512]{1,0:T(8,128)(2,1)S(1)}, u32[]{:S(2)}, u32[]{:S(2)}) collective-permute-start(bf16[512,512]{1,0:T(8,128)(2,1)} %shard_map.152.refs_2_), channel_id=1, source_target_pairs={{0,4},{4,8},{8,12},{1,5},{5,9},{9,13},{2,6},{6,10},{10,14},{3,7},{... | collective-permute-start | bytes 1572872 | tf_op jit(solution)/shard_map/ppermute | solution.py:163
  322.7 4.5 %collective-permute-done.20.refs_1_ = bf16[512,512]{1,0:T(8,128)(2,1)S(1)} collective-permute-done((bf16[512,512]{1,0:T(8,128)(2,1)}, bf16[512,512]{1,0:T(8,128)(2,1)S(1)}, u32[]{:S(2)}, u32[]{:S(2)}) %collective-permute-start.20) | collective-permute-done | bytes 524320 | tf_op jit(solution)/shard_map/ppermute | solution.py:163
  327.3 4.0 %collective-permute-done.21.refs_3_ = bf16[512,512]{1,0:T(8,128)(2,1)S(1)} collective-permute-done((bf16[512,512]{1,0:T(8,128)(2,1)}, bf16[512,512]{1,0:T(8,128)(2,1)S(1)}, u32[]{:S(2)}, u32[]{:S(2)}) %collective-permute-start.21) | collective-permute-done | bytes 524320 | tf_op jit(solution)/shard_map/ppermute | solution.py:163
  332.1 10.5 %shard_map.153 = (bf16[256,1024]{1,0:T(8,128)(2,1)}, bf16[256,1024]{1,0:T(8,128)(2,1)}) custom-call(s32[4]{0:T(128)} %broadcast_select_fusion.8.order_ref, bf16[512,256]{1,0:T(8,128)(2,1)} %shard_map.145.refs_0_, bf16[512,512]{1,0:T(8,128)(2,1)} %copy-done.10, bf16[512,512]{1,0:T(8,128)(2,1)} %shard_map.152.refs_2_, bf16[512,512]{1,0:T(8,128)(2,1)} %copy-done.11, ...), custom_call_target="tpu_custom_call" | custom-call | tf_op jit(solution)/shard_map/pallas_call | solution.py:433
  347.6 6.8 %collective-permute-done.23 = bf16[1,128,1024]{2,1,0:T(8,128)(2,1)S(1)} collective-permute-done((bf16[1,128,1024]{2,1,0:T(8,128)(2,1)S(1)}, bf16[1,128,1024]{2,1,0:T(8,128)(2,1)S(1)}, u32[]{:S(2)}, u32[]{:S(2)}) %collective-permute-start.23) | collective-permute-done | bytes 262176 | tf_op jit(solution)/shard_map/ppermute | solution.py:33
  (178 shorter events, 82.0 us)
Async XLA Ops:
  6.5 92.9 %all-gather.7.cloned.1.call-start = ((), (), s32[]{:S(2)}) async-start(), calls=%async_computation.1 | async-start | bytes 1310720 | tf_op jit(solution)/shard_map/all_gather | solution.py:329
  25.9 25.0 %collective-permute-start.2 = (bf16[1024,256]{1,0:T(8,128)(2,1)}, bf16[1024,256]{1,0:T(8,128)(2,1)}, u32[]{:S(2)}, u32[]{:S(2)}) collective-permute-start(bf16[1024,256]{1,0:T(8,128)(2,1)} %all_gather.18.refs_1_), channel_id=1, source_target_pairs={{0,16},{16,0},{1,17},{17,1},{2,18},{18,2},{3,19},{19,3},{4,20},{20... | collective-permute-start | bytes 1572872 | tf_op jit(solution)/shard_map/ppermute | solution.py:312
  43.8 17.7 %collective-permute-start.1 = (bf16[1024,256]{1,0:T(8,128)(2,1)S(1)}, bf16[1024,256]{1,0:T(8,128)(2,1)}, u32[]{:S(2)}, u32[]{:S(2)}) collective-permute-start(bf16[1024,256]{1,0:T(8,128)(2,1)S(1)} %all_gather.20.refs_1_.refs_5_), channel_id=1, source_target_pairs={{0,16},{16,0},{1,17},{17,1},{2,18},{18,2},{3,19},{19,3},{4,20},{20... | collective-permute-start | bytes 1572872 | tf_op jit(solution)/shard_map/ppermute | solution.py:312
  47.6 168.8 %all-gather.9.cloned.1.call-start = ((), (), s32[]{:S(2)}) async-start(), calls=%async_computation.2 | async-start | bytes 1310720 | tf_op jit(solution)/shard_map/all_gather | solution.py:329
  53.9 22.0 %collective-permute-start.3 = (bf16[512,512]{1,0:T(8,128)(2,1)}, bf16[512,512]{1,0:T(8,128)(2,1)S(1)}, u32[]{:S(2)}, u32[]{:S(2)}) collective-permute-start(bf16[512,512]{1,0:T(8,128)(2,1)} %shard_map.147.refs_2_), channel_id=1, source_target_pairs={{0,4},{4,8},{8,12},{1,5},{5,9},{9,13},{2,6},{6,10},{10,14},{3,7},{... | collective-permute-start | bytes 1572872 | tf_op jit(solution)/shard_map/ppermute | solution.py:163
  57.6 26.0 %collective-permute-start.4 = (bf16[512,512]{1,0:T(8,128)(2,1)}, bf16[512,512]{1,0:T(8,128)(2,1)S(1)}, u32[]{:S(2)}, u32[]{:S(2)}) collective-permute-start(bf16[512,512]{1,0:T(8,128)(2,1)} %shard_map.147.refs_2_), channel_id=1, source_target_pairs={{4,0},{8,4},{12,8},{5,1},{9,5},{13,9},{6,2},{10,6},{14,10},{7,3},{... | collective-permute-start | bytes 1572872 | tf_op jit(solution)/shard_map/ppermute | solution.py:163
  94.6 2.1 collective-permute-start.5
  97.9 14.0 %collective-permute-start.6 = (bf16[256,1024]{1,0:T(8,128)(2,1)S(1)}, bf16[256,1024]{1,0:T(8,128)(2,1)S(1)}, u32[]{:S(2)}, u32[]{:S(2)}) collective-permute-start(bf16[256,1024]{1,0:T(8,128)(2,1)S(1)} %add_convert_fusion.2), channel_id=1, source_target_pairs={{0,2},{1,3},{2,0},{3,1},{4,6},{5,7},{6,4},{7,5},{8,10},{9,11},{10,... | collective-permute-start | bytes 1572872 | tf_op jit(solution)/shard_map/ppermute | solution.py:33
  99.5 25.2 %collective-permute-start.8 = (bf16[1024,512]{1,0:T(8,128)(2,1)}, bf16[1024,512]{1,0:T(8,128)(2,1)}, u32[]{:S(2)}, u32[]{:S(2)}) collective-permute-start(bf16[1024,512]{1,0:T(8,128)(2,1)} %all-gather.7.cloned.1.call-done.refs_1_.refs_7_), channel_id=1, source_target_pairs={{0,16},{16,0},{1,17},{17,1},{2,18},{18,2},{3,19},{19,3},{4,20},{20... | collective-permute-start | bytes 3145736 | tf_op jit(solution)/shard_map/ppermute | solution.py:312
  128.5 53.4 %collective-permute-start.10 = (bf16[512,512]{1,0:T(8,128)(2,1)}, bf16[512,512]{1,0:T(8,128)(2,1)S(1)}, u32[]{:S(2)}, u32[]{:S(2)}) collective-permute-start(bf16[512,512]{1,0:T(8,128)(2,1)} %get-tuple-element.26.refs_1_), channel_id=1, source_target_pairs={{0,8},{4,12},{8,0},{12,4},{1,9},{5,13},{9,1},{13,5},{2,10},{6,14},... | collective-permute-start | bytes 1572872 | tf_op jit(solution)/shard_map/ppermute | solution.py:600
  128.9 53.1 %collective-permute-start.11 = (bf16[512,512]{1,0:T(8,128)(2,1)}, bf16[512,512]{1,0:T(8,128)(2,1)S(1)}, u32[]{:S(2)}, u32[]{:S(2)}) collective-permute-start(bf16[512,512]{1,0:T(8,128)(2,1)} %get-tuple-element.26.refs_1_), channel_id=1, source_target_pairs={{0,4},{4,8},{8,12},{12,0},{1,5},{5,9},{9,13},{13,1},{2,6},{6,10},{... | collective-permute-start | bytes 1572872 | tf_op jit(solution)/shard_map/ppermute | solution.py:600
  130.4 51.6 %collective-permute-start.9 = (bf16[512,512]{1,0:T(8,128)(2,1)}, bf16[512,512]{1,0:T(8,128)(2,1)}, u32[]{:S(2)}, u32[]{:S(2)}) collective-permute-start(bf16[512,512]{1,0:T(8,128)(2,1)} %get-tuple-element.26.refs_1_), channel_id=1, source_target_pairs={{0,12},{4,0},{8,4},{12,8},{1,13},{5,1},{9,5},{13,9},{2,14},{6,2},{... | collective-permute-start | bytes 1572872 | tf_op jit(solution)/shard_map/ppermute | solution.py:600
  132.7 103.4 %all-gather.11.cloned.1.call-start = ((), (), s32[]{:S(2)}) async-start(), calls=%async_computation.3 | async-start | bytes 1310720 | tf_op jit(solution)/shard_map/all_gather | solution.py:329
  195.2 2.1 collective-permute-start.12
  198.6 14.1 %collective-permute-start.13 = (bf16[256,1024]{1,0:T(8,128)(2,1)S(1)}, bf16[256,1024]{1,0:T(8,128)(2,1)}, u32[]{:S(2)}, u32[]{:S(2)}) collective-permute-start(bf16[256,1024]{1,0:T(8,128)(2,1)S(1)} %add_convert_fusion.1), channel_id=1, source_target_pairs={{0,2},{1,3},{2,0},{3,1},{4,6},{5,7},{6,4},{7,5},{8,10},{9,11},{10,... | collective-permute-start | bytes 1572872 | tf_op jit(solution)/shard_map/ppermute | solution.py:33
  199.2 75.3 %all-gather.5.cloned.1.call-start = ((), (), s32[]{:S(2)}) async-start(), calls=%async_computation | async-start | bytes 1310720 | tf_op jit(solution)/shard_map/all_gather | solution.py:329
  215.8 21.8 %collective-permute-start.14 = (bf16[256,1024]{1,0:T(8,128)(2,1)}, bf16[256,1024]{1,0:T(8,128)(2,1)S(1)}, u32[]{:S(2)}, u32[]{:S(2)}) collective-permute-start(bf16[256,1024]{1,0:T(8,128)(2,1)} %multiply_convert_fusion.1), channel_id=1, source_target_pairs={{0,1},{1,0},{2,3},{3,2},{4,5},{5,4},{6,7},{7,6},{8,9},{9,8},{10,11... | collective-permute-start | bytes 1572872 | tf_op jit(solution)/shard_map/ppermute | solution.py:33
  216.4 26.3 %collective-permute-start.15 = (bf16[1024,512]{1,0:T(8,128)(2,1)}, bf16[1024,512]{1,0:T(8,128)(2,1)}, u32[]{:S(2)}, u32[]{:S(2)}) collective-permute-start(bf16[1024,512]{1,0:T(8,128)(2,1)} %all-gather.9.cloned.1.call-done), channel_id=1, source_target_pairs={{0,16},{16,0},{1,17},{17,1},{2,18},{18,2},{3,19},{19,3},{4,20},{20... | collective-permute-start | bytes 3145736 | tf_op jit(solution)/shard_map/ppermute | solution.py:312
  236.1 28.6 %collective-permute-start.16 = (bf16[2048,256]{1,0:T(8,128)(2,1)}, bf16[2048,256]{1,0:T(8,128)(2,1)S(1)}, u32[]{:S(2)}, u32[]{:S(2)}) collective-permute-start(bf16[2048,256]{1,0:T(8,128)(2,1)} %all-gather.11.cloned.1.call-done.own), channel_id=1, source_target_pairs={{0,16},{16,0},{1,17},{17,1},{2,18},{18,2},{3,19},{19,3},{4,20},{20... | collective-permute-start | bytes 3145736 | tf_op jit(solution)/shard_map/ppermute | solution.py:312
  273.9 14.1 %collective-permute-start.18 = (bf16[256,1024]{1,0:T(8,128)(2,1)S(1)}, bf16[256,1024]{1,0:T(8,128)(2,1)}, u32[]{:S(2)}, u32[]{:S(2)}) collective-permute-start(bf16[256,1024]{1,0:T(8,128)(2,1)S(1)} %add_convert_fusion), channel_id=1, source_target_pairs={{0,2},{1,3},{2,0},{3,1},{4,6},{5,7},{6,4},{7,5},{8,10},{9,11},{10,... | collective-permute-start | bytes 1572872 | tf_op jit(solution)/shard_map/ppermute | solution.py:33
  274.5 25.1 %collective-permute-start = (bf16[1024,512]{1,0:T(8,128)(2,1)}, bf16[1024,512]{1,0:T(8,128)(2,1)S(1)}, u32[]{:S(2)}, u32[]{:S(2)}) collective-permute-start(bf16[1024,512]{1,0:T(8,128)(2,1)} %all-gather.5.cloned.1.call-done.refs_1_.refs_5_), channel_id=1, source_target_pairs={{0,16},{16,0},{1,17},{17,1},{2,18},{18,2},{3,19},{19,3},{4,20},{20... | collective-permute-start | bytes 3145736 | tf_op jit(solution)/shard_map/ppermute | solution.py:312
  304.0 23.3 %collective-permute-start.20 = (bf16[512,512]{1,0:T(8,128)(2,1)}, bf16[512,512]{1,0:T(8,128)(2,1)S(1)}, u32[]{:S(2)}, u32[]{:S(2)}) collective-permute-start(bf16[512,512]{1,0:T(8,128)(2,1)} %shard_map.152.refs_2_), channel_id=1, source_target_pairs={{0,4},{4,8},{8,12},{1,5},{5,9},{9,13},{2,6},{6,10},{10,14},{3,7},{... | collective-permute-start | bytes 1572872 | tf_op jit(solution)/shard_map/ppermute | solution.py:163
  316.6 14.6 %collective-permute-start.21 = (bf16[512,512]{1,0:T(8,128)(2,1)}, bf16[512,512]{1,0:T(8,128)(2,1)S(1)}, u32[]{:S(2)}, u32[]{:S(2)}) collective-permute-start(bf16[512,512]{1,0:T(8,128)(2,1)} %shard_map.152.refs_2_), channel_id=1, source_target_pairs={{4,0},{8,4},{12,8},{5,1},{9,5},{13,9},{6,2},{10,6},{14,10},{7,3},{... | collective-permute-start | bytes 1572872 | tf_op jit(solution)/shard_map/ppermute | solution.py:163
  346.0 8.4 %collective-permute-start.23 = (bf16[1,128,1024]{2,1,0:T(8,128)(2,1)S(1)}, bf16[1,128,1024]{2,1,0:T(8,128)(2,1)S(1)}, u32[]{:S(2)}, u32[]{:S(2)}) collective-permute-start(bf16[1,128,1024]{2,1,0:T(8,128)(2,1)S(1)} %fusion.34), channel_id=1, source_target_pairs={{0,2},{1,3},{2,0},{3,1},{4,6},{5,7},{6,4},{7,5},{8,10},{9,11},{10,... | collective-permute-start | bytes 786440 | tf_op jit(solution)/shard_map/ppermute | solution.py:33
  (30 other events, 171.9 us)
Sparse Core Ops, SparseCore 0:
  47.7 34.9 all-gather.6
  132.8 49.4 all-gather.8
  199.3 36.7 all-gather.10
  237.5 27.3 all-gather.4
where the time goes:
time: 364 us; the launch traced here: 363 us
  waiting for transfers between devices  178 us (49%)
  Pallas kernels  54.2 us (15%)
  starting transfers between devices  35.9 us (10%)
  blocking collectives  34.4 us (9%)
  other arithmetic  26.3 us (7%)
  between operations  13.7 us (4%)
  local copies, waits for them, and re-layouts  10.5 us (3%)
  matrix products  9.52 us (3%)
    ppermute x11, waiting for transfers between devices, exchange(): return lax.ppermute(value, axis, [(i, i ^ bit) for i in range(count)])  55.6 us
    ppermute x3, waiting for transfers between devices, paired_device(): lax.ppermute(proc_kv, 'band', route)  47.6 us
    all_gather x2, blocking collectives, band_gather(): return lax.all_gather(value, 'band', axis=0, tiled=True)  34.4 us
    pallas_call x3, Pallas kernels, attend_pair(): pl.pallas_call(functools.partial(pair_attention_kernel, pieces, keyed, o_...  32.9 us
    ppermute x6, waiting for transfers between devices, swap(): return lax.ppermute(value, 'members', [(0, 1), (1, 0)])  29.1 us
    all_gather x4, waiting for transfers between devices, band_gather(): return lax.all_gather(value, 'band', axis=0, tiled=True)  18.1 us
    pallas_call x5, Pallas kernels, project_pair(): pl.pallas_call(functools.partial(project_kernel, widths), out_shape=[jax....  16.4 us
    ppermute x2, starting transfers between devices, neighbours(): lax.ppermute(block, 'band', forward)  16.4 us
  transfers between devices with their start and end apart: 28, of which 20 were waited for; matrix products, arithmetic and copies ran while one was open for 10% of the time, Pallas kernels for 10%

commit v1 on v0

--- a/solution.py
+++ b/solution.py
@@ -306,6 +306,63 @@
 def own_half(weight, axis):
     size = weight.shape[axis] // 2
     return lax.dynamic_slice_in_dim(weight, lax.axis_index("members") * size, size, axis)
+
+
+def whole_pack(w_in, w_out, which, other):
+    member = lax.axis_index("members")
+    member = 1 - member if other else member
+    take = lambda w, axis: lax.dynamic_slice_in_dim(
+        w, member * (w.shape[axis] // 2), w.shape[axis] // 2, axis
+    )
+    parts = {name: take(w_in[i], 1) for i, name in enumerate("qkv") if name in which}
+    if "o" in which:
+        parts["o"] = stacked_columns(take(w_out, 0))
+    return jnp.concatenate([parts[name] for name in which], axis=1)
+
+
+def from_bands(value):
+    bands = lax.axis_size("band")
+    pieces = [value]
+    for step in range(1, bands):
+        pieces.append(lax.ppermute(value, "band", [(i, (i - step) % bands) for i in range(bands)]))
+    return pieces
+
+
+def placed_kernel(groups, widths, source_ref, *refs):
+    values = refs[0]
+    bands = source_ref.shape[0]
+    pieces = refs[1 : 1 + groups * bands]
+    outs = refs[1 + groups * bands :]
+    out, mats = outs[0], outs[1:]
+    for group in range(groups):
+        mat = mats[group]
+        for band in range(bands):
+            piece = pieces[group * bands + band]
+            rows = piece.shape[0]
+            start = pl.multiple_of(source_ref[band] * rows, rows)
+            mat[pl.ds(start, rows), :] = piece[...]
+    for group in range(groups):
+        out[:, group * widths : (group + 1) * widths] = dot(
+            values[...], mats[group][:, :widths]
+        ).astype(jnp.bfloat16)
+
+
+def project_placed(values, groups, widths, emit):
+    bands = lax.axis_size("band")
+    sources = (lax.axis_index("band") + jnp.arange(bands, dtype=jnp.int32)) % bands
+    rows = values.shape[0]
+    mat = (bands * groups[0][0].shape[0], groups[0][0].shape[1])
+    out = jax.ShapeDtypeStruct((rows, len(groups) * widths), jnp.bfloat16)
+    vmem = lambda: pl.BlockSpec(memory_space=pltpu.VMEM)
+    mats = [jax.ShapeDtypeStruct(mat, jnp.bfloat16)] * len(groups)
+    return pl.pallas_call(
+        functools.partial(placed_kernel, len(groups), widths),
+        in_specs=[pl.BlockSpec(memory_space=pltpu.SMEM)]
+        + [vmem() for _ in range(1 + bands * len(groups))],
+        out_specs=[vmem()] + ([vmem() for _ in groups] if emit else []),
+        out_shape=[out] + (mats if emit else []),
+        scratch_shapes=[] if emit else [pltpu.VMEM(mat, jnp.bfloat16) for _ in groups],
+    )(sources, values, *[piece for group in groups for piece in group])
 
 
 def swap(value):
@@ -492,7 +549,8 @@
 
 
 def sum_over_head(away, keep):
-    total = keep.astype(jnp.float32) + exchange(away, "head", 1).astype(jnp.float32)
+    came = exchange(away, "head", 1)
+    total = keep.astype(jnp.float32) + came.astype(jnp.float32)
     bit = 2
     while bit < lax.axis_size("head"):
         sent = total.astype(jnp.bfloat16)
@@ -562,22 +620,17 @@
     kv_cols, q_cols = (0, 2 * LANES), (2 * LANES, LANES)
     o_start = 3 * LANES
 
-    enc_kv_own = band_gather(pack(enc_in, enc_out, "kv"))
-    enc_kv_other = swap(enc_kv_own)
-    enc_qo_own = band_gather(barrier((pack(enc_in, enc_out, "qo"), enc_kv_own))[0])
-    enc_qo_other = swap(enc_qo_own)
-    packed = (
-        pack(proc_in, proc_out, "kvqo"),
-        own_half(ff_up, 1),
-        own_half(ff_down, 0),
-        pack(dec_in, dec_out, "kvqo"),
-    )
-    packed = barrier(packed + (enc_kv_own,))[:4]
-    proc_own, up_own, down_own, dec_own = [band_gather(value) for value in packed]
+    enc_kv_pieces = from_bands(
+        jnp.concatenate([whole_pack(enc_in, enc_out, "kv", o) for o in (False, True)], axis=1),
+    )
+    enc_qo_own = from_bands(whole_pack(enc_in, enc_out, "qo", False))
+    enc_qo_other = [whole_pack(enc_in, enc_out, "qo", True)]
+    for piece in enc_qo_own[1:]:
+        enc_qo_other.append(swap(piece))
+    early = barrier((pack(proc_in, proc_out, "kvqo"), own_half(ff_up, 1), *enc_kv_pieces[1:]))
+    proc_own, up_own = [band_gather(value) for value in early[:2]]
     proc_other = swap(proc_own)
     up_other = swap(up_own)
-    down_other = swap(down_own)
-    dec_other = swap(dec_own)
 
     enc_bias = list_bias(enc_list, enc_count, band_index, mesh_blocks, grid_blocks)
     dec_bias = list_bias(dec_list, dec_count, band_index, grid_blocks, mesh_blocks)
@@ -587,17 +640,24 @@
     grid_norm = normed(grid_feats)
     mesh_norm = normed(mesh_feats)
 
-    (enc_kv,) = project_pair(grid_norm, enc_kv_own, enc_kv_other, [kv_cols])
+    (enc_kv,) = project_placed(grid_norm, [enc_kv_pieces], 4 * LANES, False)
     low, high = neighbours(enc_kv)
-    (enc_q,) = project_pair(mesh_norm, enc_qo_own, enc_qo_other, [(0, LANES)])
+    enc_q, qo_own, qo_other = project_placed(
+        mesh_norm, [enc_qo_own, enc_qo_other], LANES, True
+    )
     away, keep = attend_pair(
-        enc_q, [low, enc_kv, high], [enc_bias], False, [enc_qo_own, enc_qo_other], LANES, order
+        enc_q, [low, enc_kv, high], [enc_bias], False, [qo_own, qo_other], LANES, order
     )
     state = half_of(mesh_feats, side).astype(jnp.float32) + sum_over_head(away, keep)
 
     proc_norm = both_halves(normed(state), side)
     proc_kv, proc_q = project_pair(proc_norm, proc_own, proc_other, [kv_cols, q_cols])
     slab = [proc_kv] + [lax.ppermute(proc_kv, "band", route) for route in routes]
+    late = barrier((own_half(ff_down, 0), pack(dec_in, dec_out, "kvqo"), *slab[1:]))
+    down_own = band_gather(late[0])
+    down_other = swap(down_own)
+    dec_own = band_gather(late[1])
+    dec_other = swap(dec_own)
     away, keep = attend_pair(
         proc_q, slab, [query_ids, key_ids], True, [proc_own, proc_other], o_start, order
     )

time: 364 us -> 369 us (1.014)
  blocking collectives: 34.4 us -> 0 us
  waiting for transfers between devices: 178 us -> 205 us
  starting transfers between devices: 35.9 us -> 45.6 us
    all_gather x2 -> x0, blocking collectives: 34.4 us -> none  [band_gather(): return lax.all_gather(value, 'band', axis=0, tiled=True)]
    ppermute x6 -> x7, waiting for transfers between devices: 29.1 us -> 49.4 us  [swap(): return lax.ppermute(value, 'members', [(0, 1), (1, 0)])]
    ppermute x0 -> x6, starting transfers between devices: none -> 16.8 us  [from_bands(): lax.ppermute(value, 'band', [(i, (i - step) % bands) for i in range(bands)])]
    ppermute x0 -> x6, waiting for transfers between devices: none -> 11.7 us  [from_bands(): lax.ppermute(value, 'band', [(i, (i - step) % bands) for i in range(bands)])]
    ppermute x2, waiting for transfers between devices: 16 us -> 4.33 us  [neighbours(): lax.ppermute(block, 'band', forward)]
    ppermute x3, waiting for transfers between devices: 47.6 us -> 57.7 us  [paired_device(): lax.ppermute(proc_kv, 'band', route)]
    ppermute x2, starting transfers between devices: 16.4 us -> 6.72 us  [neighbours(): lax.ppermute(block, 'band', forward)]
    ppermute x2, waiting for transfers between devices: 11.7 us -> 4.76 us  [neighbours(): lax.ppermute(block, 'band', backward)]
  transfers between devices with their start and end apart: 28 -> 35, of which waited for: 20 -> 22; matrix products, arithmetic and copies ran while one was open for 10% -> 11% of each run, Pallas kernels for 10% -> 7%
where the time goes in v1:
time: 369 us; the launch traced here: 368 us
  waiting for transfers between devices  205 us (56%)
  Pallas kernels  54.5 us (15%)
  starting transfers between devices  45.6 us (12%)
  other arithmetic  26.4 us (7%)
  between operations  13.7 us (4%)
  local copies, waits for them, and re-layouts  12.5 us (3%)
  matrix products  10.6 us (3%)
    ppermute x3, waiting for transfers between devices, paired_device(): lax.ppermute(proc_kv, 'band', route)  57.7 us
    ppermute x11, waiting for transfers between devices, exchange(): return lax.ppermute(value, axis, [(i, i ^ bit) for i in range(count)])  52.8 us
    ppermute x7, waiting for transfers between devices, swap(): return lax.ppermute(value, 'members', [(0, 1), (1, 0)])  49.4 us
    pallas_call x3, Pallas kernels, attend_pair(): pl.pallas_call(functools.partial(pair_attention_kernel, pieces, keyed, o_...  33 us
    all_gather x4, waiting for transfers between devices, band_gather(): return lax.all_gather(value, 'band', axis=0, tiled=True)  24.1 us
    ppermute x6, starting transfers between devices, from_bands(): lax.ppermute(value, 'band', [(i, (i - step) % bands) for i in range(bands)])  16.8 us
    ppermute x6, waiting for transfers between devices, from_bands(): lax.ppermute(value, 'band', [(i, (i - step) % bands) for i in range(bands)])  11.7 us
    dot_general x2, matrix products, dot(): return jnp.dot(a, b, preferred_element_type=jnp.float32)  10.6 us
  transfers between devices with their start and end apart: 35, of which 22 were waited for; matrix products, arithmetic and copies ran while one was open for 11% of the time, Pallas kernels for 7%

profile of v1, /device:TPU:0, one launch (start us, length us, event | category | flops | bytes accessed | tf_op | source)
XLA Modules:
  0.0 368.1 jit_solution(3332013042746077890)
XLA Ops:
  7.8 5.1 %collective-permute-start.6 = (bf16[256,512]{1,0:T(8,128)(2,1)S(1)}, bf16[256,512]{1,0:T(8,128)(2,1)}, u32[]{:S(2)}, u32[]{:S(2)}) collective-permute-start(bf16[256,512]{1,0:T(8,128)(2,1)S(1)} %pad_maximum_fusion.9.refs_1_), channel_id=1, source_target_pairs={{0,12},{4,0},{8,4},{12,8},{1,13},{5,1},{9,5},{13,9},{2,14},{6,2},{... | collective-permute-start | bytes 786440 | tf_op jit(solution)/shard_map/ppermute | solution.py:327
  23.7 6.7 %collective-permute-start.2 = (bf16[256,256]{1,0:T(8,128)(2,1)S(1)}, bf16[256,256]{1,0:T(8,128)(2,1)}, u32[]{:S(2)}, u32[]{:S(2)}) collective-permute-start(bf16[256,256]{1,0:T(8,128)(2,1)S(1)} %maximum_maximum_fusion.2.refs_1_), channel_id=1, source_target_pairs={{0,4},{4,8},{8,12},{12,0},{1,5},{5,9},{9,13},{13,1},{2,6},{6,10},{... | collective-permute-start | bytes 393224 | tf_op jit(solution)/shard_map/ppermute | solution.py:327
  30.4 11.7 %collective-permute-done.7.refs_3_ = bf16[256,512]{1,0:T(8,128)(2,1)} collective-permute-done((bf16[256,512]{1,0:T(8,128)(2,1)S(1)}, bf16[256,512]{1,0:T(8,128)(2,1)}, u32[]{:S(2)}, u32[]{:S(2)}) %collective-permute-start.7) | collective-permute-done | bytes 262176 | tf_op jit(solution)/shard_map/ppermute | solution.py:327
  46.5 4.6 %collective-permute-start.9 = (bf16[512,512]{1,0:T(8,128)(2,1)}, bf16[512,512]{1,0:T(8,128)(2,1)S(1)}, u32[]{:S(2)}, u32[]{:S(2)}) collective-permute-start(bf16[512,512]{1,0:T(8,128)(2,1)} %shard_map.146.refs_2_), channel_id=1, source_target_pairs={{0,4},{4,8},{8,12},{1,5},{5,9},{9,13},{2,6},{6,10},{10,14},{3,7},{... | collective-permute-start | bytes 1572872 | tf_op jit(solution)/shard_map/ppermute | solution.py:163
  64.6 10.2 %shard_map.147 = (bf16[256,1024]{1,0:T(8,128)(2,1)}, bf16[256,1024]{1,0:T(8,128)(2,1)}) custom-call(s32[4]{0:T(128)} %and_select_fusion.1.order_ref, bf16[512,256]{1,0:T(8,128)(2,1)} %get-tuple-element.22.refs_0_, bf16[512,512]{1,0:T(8,128)(2,1)} %copy-done.11, bf16[512,512]{1,0:T(8,128)(2,1)} %shard_map.146.refs_2_, bf16[512,512]{1,0:T(8,128)(2,1)} %copy-done.10, ...), custom_call_target="tpu_custom_call" | custom-call | tf_op jit(solution)/shard_map/pallas_call | solution.py:490
  79.0 12.8 %collective-permute-done.12 = bf16[256,1024]{1,0:T(8,128)(2,1)S(1)} collective-permute-done((bf16[256,1024]{1,0:T(8,128)(2,1)S(1)}, bf16[256,1024]{1,0:T(8,128)(2,1)S(1)}, u32[]{:S(2)}, u32[]{:S(2)}) %collective-permute-start.12) | collective-permute-done | bytes 524320 | tf_op jit(solution)/shard_map/ppermute | solution.py:33
  92.4 13.7 %all-gather.5.cloned.1.call-done.refs_1_.refs_7_ = bf16[1024,512]{1,0:T(8,128)(2,1)} async-done(((bf16[256,512]{1,0:T(8,128)(2,1)}), bf16[1024,512]{1,0:T(8,128)(2,1)}) %all-gather.5.cloned.1.call-update) | async-done | bytes 1048592 | tf_op jit(solution)/shard_map/all_gather | solution.py:386
  112.2 18.7 %collective-permute-done.14.refs_2_.refs_8_ = bf16[1024,512]{1,0:T(8,128)(2,1)} collective-permute-done((bf16[1024,512]{1,0:T(8,128)(2,1)}, bf16[1024,512]{1,0:T(8,128)(2,1)}, u32[]{:S(2)}, u32[]{:S(2)}) %collective-permute-start.14) | collective-permute-done | bytes 1048608 | tf_op jit(solution)/shard_map/ppermute | solution.py:369
  140.4 11.6 %collective-permute-done.15.refs_2_ = bf16[512,512]{1,0:T(8,128)(2,1)S(1)} collective-permute-done((bf16[512,512]{1,0:T(8,128)(2,1)}, bf16[512,512]{1,0:T(8,128)(2,1)S(1)}, u32[]{:S(2)}, u32[]{:S(2)}) %collective-permute-start.15) | collective-permute-done | bytes 524320 | tf_op jit(solution)/shard_map/ppermute | solution.py:655
  152.0 46.0 %collective-permute-done.16.refs_3_ = bf16[512,512]{1,0:T(8,128)(2,1)S(1)} collective-permute-done((bf16[512,512]{1,0:T(8,128)(2,1)}, bf16[512,512]{1,0:T(8,128)(2,1)S(1)}, u32[]{:S(2)}, u32[]{:S(2)}) %collective-permute-start.16) | collective-permute-done | bytes 524320 | tf_op jit(solution)/shard_map/ppermute | solution.py:655
  198.8 12.3 %shard_map.150 = (bf16[256,1024]{1,0:T(8,128)(2,1)}, bf16[256,1024]{1,0:T(8,128)(2,1)}) custom-call(s32[4]{0:T(128)} %and_select_fusion.1.order_ref, bf16[512,256]{1,0:T(8,128)(2,1)} %get-tuple-element.30.refs_0_, bf16[512,512]{1,0:T(8,128)(2,1)} %get-tuple-element.28.refs_1_, bf16[512,512]{1,0:T(8,128)(2,1)} %copy-done.8, bf16[512,512]{1,0:T(8,128)(2,1)} %copy-done.9, ...), custom_call_target="tpu_custom_call" | custom-call | tf_op jit(solution)/shard_map/pallas_call | solution.py:490
  216.7 11.0 %collective-permute-done.20 = bf16[256,1024]{1,0:T(8,128)(2,1)} collective-permute-done((bf16[256,1024]{1,0:T(8,128)(2,1)S(1)}, bf16[256,1024]{1,0:T(8,128)(2,1)}, u32[]{:S(2)}, u32[]{:S(2)}) %collective-permute-start.20) | collective-permute-done | bytes 524320 | tf_op jit(solution)/shard_map/ppermute | solution.py:33
  233.4 10.3 %all-gather.11.cloned.1.call-done.own = bf16[2048,256]{1,0:T(8,128)(2,1)} async-done(((bf16[512,256]{1,0:T(8,128)(2,1)}), bf16[2048,256]{1,0:T(8,128)(2,1)}) %all-gather.11.cloned.1.call-update) | async-done | bytes 1048592 | tf_op jit(solution)/shard_map/all_gather | solution.py:386
  245.2 5.2 %fusion.10.own_hidden = bf16[512,512]{1,0:T(8,128)(2,1)} fusion(bf16[1024,512]{1,0:T(8,128)(2,1)} %all-gather.9.cloned.1.call-done, bf16[256,1024]{1,0:T(8,128)(2,1)} %get-tuple-element.46, bf16[256,1024]{1,0:T(8,128)(2,1)} %get-tuple-element.45), kind=kOutput, calls=%fused_computation.16 | convolution fusion | flops 556007424 | bytes 2621440 | tf_op jit(solution)/shard_map/dot_general | solution.py:21
  250.5 6.5 %collective-permute-done.22 = bf16[1024,512]{1,0:T(8,128)(2,1)} collective-permute-done((bf16[1024,512]{1,0:T(8,128)(2,1)}, bf16[1024,512]{1,0:T(8,128)(2,1)}, u32[]{:S(2)}, u32[]{:S(2)}) %collective-permute-start.22) | collective-permute-done | bytes 1048608 | tf_op jit(solution)/shard_map/ppermute | solution.py:369
  257.0 5.3 %fusion.13.other_hidden = bf16[512,512]{1,0:T(8,128)(2,1)} fusion(bf16[1024,512]{1,0:T(8,128)(2,1)} %collective-permute-done.22, bf16[256,1024]{1,0:T(8,128)(2,1)S(1)} %copy-done.17, bf16[256,1024]{1,0:T(8,128)(2,1)S(1)} %copy-done.16), kind=kOutput, calls=%fused_computation.19 | convolution fusion | flops 556007424 | bytes 2621440 | tf_op jit(solution)/shard_map/dot_general | solution.py:21
  262.3 16.6 %collective-permute-done.23.other = bf16[2048,256]{1,0:T(8,128)(2,1)S(1)} collective-permute-done((bf16[2048,256]{1,0:T(8,128)(2,1)}, bf16[2048,256]{1,0:T(8,128)(2,1)S(1)}, u32[]{:S(2)}, u32[]{:S(2)}) %collective-permute-start.23) | collective-permute-done | bytes 1048608 | tf_op jit(solution)/shard_map/ppermute | solution.py:369
  279.9 4.9 %shard_map.151 = (bf16[256,1024]{1,0:T(8,128)(2,1)}, bf16[256,1024]{1,0:T(8,128)(2,1)}) custom-call(s32[2]{0:T(128)} %pad_add_fusion.1.order_ref, bf16[512,512]{1,0:T(8,128)(2,1)} %fusion.10.own_hidden, bf16[512,512]{1,0:T(8,128)(2,1)} %fusion.13.other_hidden, bf16[2048,256]{1,0:T(8,128)(2,1)} %all-gather.11.cloned.1.call-done.own, bf16[2048,256]{1,0:T(8,128)(2,1)} %copy-done.6), custom_call_target="tpu_custom_call" | custom-call | tf_op jit(solution)/shard_map/pallas_call | solution.py:538
  291.1 11.1 %collective-permute-done.25 = bf16[256,1024]{1,0:T(8,128)(2,1)} collective-permute-done((bf16[256,1024]{1,0:T(8,128)(2,1)S(1)}, bf16[256,1024]{1,0:T(8,128)(2,1)}, u32[]{:S(2)}, u32[]{:S(2)}) %collective-permute-start.25) | collective-permute-done | bytes 524320 | tf_op jit(solution)/shard_map/ppermute | solution.py:33
  309.4 5.4 %collective-permute-done.18.refs_2_.refs_6_ = bf16[1024,512]{1,0:T(8,128)(2,1)S(1)} collective-permute-done((bf16[1024,512]{1,0:T(8,128)(2,1)}, bf16[1024,512]{1,0:T(8,128)(2,1)S(1)}, u32[]{:S(2)}, u32[]{:S(2)}) %collective-permute-start.18) | collective-permute-done | bytes 1048608 | tf_op jit(solution)/shard_map/ppermute | solution.py:369
  327.6 4.3 %collective-permute-done.27.refs_1_ = bf16[512,512]{1,0:T(8,128)(2,1)S(1)} collective-permute-done((bf16[512,512]{1,0:T(8,128)(2,1)}, bf16[512,512]{1,0:T(8,128)(2,1)S(1)}, u32[]{:S(2)}, u32[]{:S(2)}) %collective-permute-start.27) | collective-permute-done | bytes 524320 | tf_op jit(solution)/shard_map/ppermute | solution.py:163
  331.9 4.8 %collective-permute-done.28.refs_3_ = bf16[512,512]{1,0:T(8,128)(2,1)S(1)} collective-permute-done((bf16[512,512]{1,0:T(8,128)(2,1)}, bf16[512,512]{1,0:T(8,128)(2,1)S(1)}, u32[]{:S(2)}, u32[]{:S(2)}) %collective-permute-start.28) | collective-permute-done | bytes 524320 | tf_op jit(solution)/shard_map/ppermute | solution.py:163
  337.5 10.5 %shard_map.153 = (bf16[256,1024]{1,0:T(8,128)(2,1)}, bf16[256,1024]{1,0:T(8,128)(2,1)}) custom-call(s32[4]{0:T(128)} %broadcast_select_fusion.8.order_ref, bf16[512,256]{1,0:T(8,128)(2,1)} %shard_map.149.refs_0_, bf16[512,512]{1,0:T(8,128)(2,1)} %copy-done.13, bf16[512,512]{1,0:T(8,128)(2,1)} %shard_map.152.refs_2_, bf16[512,512]{1,0:T(8,128)(2,1)} %copy-done.14, ...), custom_call_target="tpu_custom_call" | custom-call | tf_op jit(solution)/shard_map/pallas_call | solution.py:490
  352.0 7.7 %collective-permute-done.30 = bf16[1,128,1024]{2,1,0:T(8,128)(2,1)S(1)} collective-permute-done((bf16[1,128,1024]{2,1,0:T(8,128)(2,1)S(1)}, bf16[1,128,1024]{2,1,0:T(8,128)(2,1)S(1)}, u32[]{:S(2)}, u32[]{:S(2)}) %collective-permute-start.30) | collective-permute-done | bytes 262176 | tf_op jit(solution)/shard_map/ppermute | solution.py:33
  (206 shorter events, 97.3 us)
Async XLA Ops:
  6.5 99.6 %all-gather.5.cloned.1.call-start = ((), (), s32[]{:S(2)}) async-start(), calls=%async_computation | async-start | bytes 1310720 | tf_op jit(solution)/shard_map/all_gather | solution.py:386
  7.8 15.9 %collective-permute-start.6 = (bf16[256,512]{1,0:T(8,128)(2,1)S(1)}, bf16[256,512]{1,0:T(8,128)(2,1)}, u32[]{:S(2)}, u32[]{:S(2)}) collective-permute-start(bf16[256,512]{1,0:T(8,128)(2,1)S(1)} %pad_maximum_fusion.9.refs_1_), channel_id=1, source_target_pairs={{0,12},{4,0},{8,4},{12,8},{1,13},{5,1},{9,5},{13,9},{2,14},{6,2},{... | collective-permute-start | bytes 786440 | tf_op jit(solution)/shard_map/ppermute | solution.py:327
  12.9 29.2 %collective-permute-start.7 = (bf16[256,512]{1,0:T(8,128)(2,1)S(1)}, bf16[256,512]{1,0:T(8,128)(2,1)}, u32[]{:S(2)}, u32[]{:S(2)}) collective-permute-start(bf16[256,512]{1,0:T(8,128)(2,1)S(1)} %pad_maximum_fusion.9.refs_1_), channel_id=1, source_target_pairs={{0,8},{4,12},{8,0},{12,4},{1,9},{5,13},{9,1},{13,5},{2,10},{6,14},... | collective-permute-start | bytes 786440 | tf_op jit(solution)/shard_map/ppermute | solution.py:327
  12.9 29.2 %collective-permute-start.8 = (bf16[256,512]{1,0:T(8,128)(2,1)S(1)}, bf16[256,512]{1,0:T(8,128)(2,1)}, u32[]{:S(2)}, u32[]{:S(2)}) collective-permute-start(bf16[256,512]{1,0:T(8,128)(2,1)S(1)} %pad_maximum_fusion.9.refs_1_), channel_id=1, source_target_pairs={{0,4},{4,8},{8,12},{12,0},{1,5},{5,9},{9,13},{13,1},{2,6},{6,10},{... | collective-permute-start | bytes 786440 | tf_op jit(solution)/shard_map/ppermute | solution.py:327
  14.6 36.5 %collective-permute-start = (bf16[256,256]{1,0:T(8,128)(2,1)S(1)}, bf16[256,256]{1,0:T(8,128)(2,1)}, u32[]{:S(2)}, u32[]{:S(2)}) collective-permute-start(bf16[256,256]{1,0:T(8,128)(2,1)S(1)} %maximum_maximum_fusion.2.refs_1_), channel_id=1, source_target_pairs={{0,12},{4,0},{8,4},{12,8},{1,13},{5,1},{9,5},{13,9},{2,14},{6,2},{... | collective-permute-start | bytes 393224 | tf_op jit(solution)/shard_map/ppermute | solution.py:327
  17.5 35.3 %collective-permute-start.1 = (bf16[256,256]{1,0:T(8,128)(2,1)S(1)}, bf16[256,256]{1,0:T(8,128)(2,1)}, u32[]{:S(2)}, u32[]{:S(2)}) collective-permute-start(bf16[256,256]{1,0:T(8,128)(2,1)S(1)} %maximum_maximum_fusion.2.refs_1_), channel_id=1, source_target_pairs={{0,8},{4,12},{8,0},{12,4},{1,9},{5,13},{9,1},{13,5},{2,10},{6,14},... | collective-permute-start | bytes 393224 | tf_op jit(solution)/shard_map/ppermute | solution.py:327
  23.7 29.6 %collective-permute-start.2 = (bf16[256,256]{1,0:T(8,128)(2,1)S(1)}, bf16[256,256]{1,0:T(8,128)(2,1)}, u32[]{:S(2)}, u32[]{:S(2)}) collective-permute-start(bf16[256,256]{1,0:T(8,128)(2,1)S(1)} %maximum_maximum_fusion.2.refs_1_), channel_id=1, source_target_pairs={{0,4},{4,8},{8,12},{12,0},{1,5},{5,9},{9,13},{13,1},{2,6},{6,10},{... | collective-permute-start | bytes 393224 | tf_op jit(solution)/shard_map/ppermute | solution.py:327
  45.2 18.3 %collective-permute-start.10 = (bf16[512,512]{1,0:T(8,128)(2,1)}, bf16[512,512]{1,0:T(8,128)(2,1)S(1)}, u32[]{:S(2)}, u32[]{:S(2)}) collective-permute-start(bf16[512,512]{1,0:T(8,128)(2,1)} %shard_map.146.refs_2_), channel_id=1, source_target_pairs={{4,0},{8,4},{12,8},{5,1},{9,5},{13,9},{6,2},{10,6},{14,10},{7,3},{... | collective-permute-start | bytes 1572872 | tf_op jit(solution)/shard_map/ppermute | solution.py:163
  46.5 17.1 %collective-permute-start.9 = (bf16[512,512]{1,0:T(8,128)(2,1)}, bf16[512,512]{1,0:T(8,128)(2,1)S(1)}, u32[]{:S(2)}, u32[]{:S(2)}) collective-permute-start(bf16[512,512]{1,0:T(8,128)(2,1)} %shard_map.146.refs_2_), channel_id=1, source_target_pairs={{0,4},{4,8},{8,12},{1,5},{5,9},{9,13},{2,6},{6,10},{10,14},{3,7},{... | collective-permute-start | bytes 1572872 | tf_op jit(solution)/shard_map/ppermute | solution.py:163
  77.2 153.5 %all-gather.9.cloned.1.call-start = ((), (), s32[]{:S(2)}) async-start(), calls=%async_computation.2 | async-start | bytes 1310720 | tf_op jit(solution)/shard_map/all_gather | solution.py:386
  77.4 14.3 %collective-permute-start.12 = (bf16[256,1024]{1,0:T(8,128)(2,1)S(1)}, bf16[256,1024]{1,0:T(8,128)(2,1)S(1)}, u32[]{:S(2)}, u32[]{:S(2)}) collective-permute-start(bf16[256,1024]{1,0:T(8,128)(2,1)S(1)} %add_convert_fusion.2), channel_id=1, source_target_pairs={{0,2},{1,3},{2,0},{3,1},{4,6},{5,7},{6,4},{7,5},{8,10},{9,11},{10,... | collective-permute-start | bytes 1572872 | tf_op jit(solution)/shard_map/ppermute | solution.py:33
  106.2 24.7 %collective-permute-start.14 = (bf16[1024,512]{1,0:T(8,128)(2,1)}, bf16[1024,512]{1,0:T(8,128)(2,1)}, u32[]{:S(2)}, u32[]{:S(2)}) collective-permute-start(bf16[1024,512]{1,0:T(8,128)(2,1)} %all-gather.5.cloned.1.call-done.refs_1_.refs_7_), channel_id=1, source_target_pairs={{0,16},{16,0},{1,17},{17,1},{2,18},{18,2},{3,19},{19,3},{4,20},{20... | collective-permute-start | bytes 3145736 | tf_op jit(solution)/shard_map/ppermute | solution.py:369
  134.7 17.3 %collective-permute-start.15 = (bf16[512,512]{1,0:T(8,128)(2,1)}, bf16[512,512]{1,0:T(8,128)(2,1)S(1)}, u32[]{:S(2)}, u32[]{:S(2)}) collective-permute-start(bf16[512,512]{1,0:T(8,128)(2,1)} %get-tuple-element.28.refs_1_), channel_id=1, source_target_pairs={{0,12},{4,0},{8,4},{12,8},{1,13},{5,1},{9,5},{13,9},{2,14},{6,2},{... | collective-permute-start | bytes 1572872 | tf_op jit(solution)/shard_map/ppermute | solution.py:655
  136.8 61.2 %collective-permute-start.16 = (bf16[512,512]{1,0:T(8,128)(2,1)}, bf16[512,512]{1,0:T(8,128)(2,1)S(1)}, u32[]{:S(2)}, u32[]{:S(2)}) collective-permute-start(bf16[512,512]{1,0:T(8,128)(2,1)} %get-tuple-element.28.refs_1_), channel_id=1, source_target_pairs={{0,8},{4,12},{8,0},{12,4},{1,9},{5,13},{9,1},{13,5},{2,10},{6,14},... | collective-permute-start | bytes 1572872 | tf_op jit(solution)/shard_map/ppermute | solution.py:655
  137.3 60.8 %collective-permute-start.17 = (bf16[512,512]{1,0:T(8,128)(2,1)}, bf16[512,512]{1,0:T(8,128)(2,1)}, u32[]{:S(2)}, u32[]{:S(2)}) collective-permute-start(bf16[512,512]{1,0:T(8,128)(2,1)} %get-tuple-element.28.refs_1_), channel_id=1, source_target_pairs={{0,4},{4,8},{8,12},{12,0},{1,5},{5,9},{9,13},{13,1},{2,6},{6,10},{... | collective-permute-start | bytes 1572872 | tf_op jit(solution)/shard_map/ppermute | solution.py:655
  138.6 105.2 %all-gather.11.cloned.1.call-start = ((), (), s32[]{:S(2)}) async-start(), calls=%async_computation.3 | async-start | bytes 1310720 | tf_op jit(solution)/shard_map/all_gather | solution.py:386
  213.6 14.1 %collective-permute-start.20 = (bf16[256,1024]{1,0:T(8,128)(2,1)S(1)}, bf16[256,1024]{1,0:T(8,128)(2,1)}, u32[]{:S(2)}, u32[]{:S(2)}) collective-permute-start(bf16[256,1024]{1,0:T(8,128)(2,1)S(1)} %add_convert_fusion.1), channel_id=1, source_target_pairs={{0,2},{1,3},{2,0},{3,1},{4,6},{5,7},{6,4},{7,5},{8,10},{9,11},{10,... | collective-permute-start | bytes 1572872 | tf_op jit(solution)/shard_map/ppermute | solution.py:33
  216.7 72.9 %all-gather.7.cloned.1.call-start = ((), (), s32[]{:S(2)}) async-start(), calls=%async_computation.1 | async-start | bytes 1310720 | tf_op jit(solution)/shard_map/all_gather | solution.py:386
  230.6 26.3 %collective-permute-start.22 = (bf16[1024,512]{1,0:T(8,128)(2,1)}, bf16[1024,512]{1,0:T(8,128)(2,1)}, u32[]{:S(2)}, u32[]{:S(2)}) collective-permute-start(bf16[1024,512]{1,0:T(8,128)(2,1)} %all-gather.9.cloned.1.call-done), channel_id=1, source_target_pairs={{0,16},{16,0},{1,17},{17,1},{2,18},{18,2},{3,19},{19,3},{4,20},{20... | collective-permute-start | bytes 3145736 | tf_op jit(solution)/shard_map/ppermute | solution.py:369
  243.8 35.1 %collective-permute-start.23 = (bf16[2048,256]{1,0:T(8,128)(2,1)}, bf16[2048,256]{1,0:T(8,128)(2,1)S(1)}, u32[]{:S(2)}, u32[]{:S(2)}) collective-permute-start(bf16[2048,256]{1,0:T(8,128)(2,1)} %all-gather.11.cloned.1.call-done.own), channel_id=1, source_target_pairs={{0,16},{16,0},{1,17},{17,1},{2,18},{18,2},{3,19},{19,3},{4,20},{20... | collective-permute-start | bytes 3145736 | tf_op jit(solution)/shard_map/ppermute | solution.py:369
  288.1 14.1 %collective-permute-start.25 = (bf16[256,1024]{1,0:T(8,128)(2,1)S(1)}, bf16[256,1024]{1,0:T(8,128)(2,1)}, u32[]{:S(2)}, u32[]{:S(2)}) collective-permute-start(bf16[256,1024]{1,0:T(8,128)(2,1)S(1)} %add_convert_fusion), channel_id=1, source_target_pairs={{0,2},{1,3},{2,0},{3,1},{4,6},{5,7},{6,4},{7,5},{8,10},{9,11},{10,... | collective-permute-start | bytes 1572872 | tf_op jit(solution)/shard_map/ppermute | solution.py:33
  289.6 25.1 %collective-permute-start.18 = (bf16[1024,512]{1,0:T(8,128)(2,1)}, bf16[1024,512]{1,0:T(8,128)(2,1)S(1)}, u32[]{:S(2)}, u32[]{:S(2)}) collective-permute-start(bf16[1024,512]{1,0:T(8,128)(2,1)} %all-gather.7.cloned.1.call-done.refs_1_.refs_5_), channel_id=1, source_target_pairs={{0,16},{16,0},{1,17},{17,1},{2,18},{18,2},{3,19},{19,3},{4,20},{20... | collective-permute-start | bytes 3145736 | tf_op jit(solution)/shard_map/ppermute | solution.py:369
  319.1 12.8 %collective-permute-start.27 = (bf16[512,512]{1,0:T(8,128)(2,1)}, bf16[512,512]{1,0:T(8,128)(2,1)S(1)}, u32[]{:S(2)}, u32[]{:S(2)}) collective-permute-start(bf16[512,512]{1,0:T(8,128)(2,1)} %shard_map.152.refs_2_), channel_id=1, source_target_pairs={{0,4},{4,8},{8,12},{1,5},{5,9},{9,13},{2,6},{6,10},{10,14},{3,7},{... | collective-permute-start | bytes 1572872 | tf_op jit(solution)/shard_map/ppermute | solution.py:163
  321.3 15.4 %collective-permute-start.28 = (bf16[512,512]{1,0:T(8,128)(2,1)}, bf16[512,512]{1,0:T(8,128)(2,1)S(1)}, u32[]{:S(2)}, u32[]{:S(2)}) collective-permute-start(bf16[512,512]{1,0:T(8,128)(2,1)} %shard_map.152.refs_2_), channel_id=1, source_target_pairs={{4,0},{8,4},{12,8},{5,1},{9,5},{13,9},{6,2},{10,6},{14,10},{7,3},{... | collective-permute-start | bytes 1572872 | tf_op jit(solution)/shard_map/ppermute | solution.py:163
  (43 other events, 318.8 us)
Sparse Core Ops, SparseCore 0:
  77.3 28.8 all-gather.4
  138.7 57.1 all-gather.8
  216.8 26.9 all-gather.10
  245.2 27.3 all-gather.6

commit v2 on v1

--- a/solution.py
+++ b/solution.py
@@ -26,6 +26,10 @@
     centred = values - jnp.mean(values, axis=-1, keepdims=True)
     variance = jnp.mean(centred * centred, axis=-1, keepdims=True)
     return (centred * lax.rsqrt(variance + EPSILON)).astype(jnp.bfloat16)
+
+
+def gelu(values):
+    return 0.5 * values * (1.0 + lax.erf(values * 2.0 ** (-0.5)))
 
 
 def exchange(value, axis, bit):
@@ -386,61 +390,74 @@
     return lax.all_gather(value, "band", axis=0, tiled=True)
 
 
-def project_kernel(widths, *refs):
-    source, own, other = refs[:3]
-    for (start, width), out in zip(widths, refs[3:]):
-        for place, weight in enumerate((own, other)):
-            out[:, place * width : (place + 1) * width] = dot(
-                source[...], weight[:, start : start + width]
-            ).astype(jnp.bfloat16)
-
-
-def project_pair(source, own, other, widths):
-    rows = source.shape[0]
+def project_kernel(widths, side_ref, *refs):
+    mine, theirs, own, other = refs[:4]
+    rows = mine.shape[0]
+    for half, place in ((mine, side_ref[0]), (theirs, 1 - side_ref[0])):
+        start = pl.multiple_of(place * rows, rows)
+        for (first, width), out in zip(widths, refs[4:]):
+            for group, weight in enumerate((own, other)):
+                out[pl.ds(start, rows), group * width : (group + 1) * width] = dot(
+                    half[...], weight[:, first : first + width]
+                ).astype(jnp.bfloat16)
+
+
+def project_pair(mine, theirs, side, own, other, widths):
+    rows = 2 * mine.shape[0]
+    vmem = lambda: pl.BlockSpec(memory_space=pltpu.VMEM)
     return pl.pallas_call(
         functools.partial(project_kernel, widths),
+        in_specs=[pl.BlockSpec(memory_space=pltpu.SMEM)] + [vmem() for _ in range(4)],
+        out_specs=[vmem() for _ in widths],
         out_shape=[jax.ShapeDtypeStruct((rows, 2 * w), jnp.bfloat16) for _, w in widths],
-    )(source, own, other)
+    )(side.reshape(1).astype(jnp.int32), mine, theirs, own, other)
 
 
 def pair_attention_kernel(pieces, keyed, o_start, order_ref, *refs):
-    q_ref = refs[0]
-    kv_refs = refs[1 : 1 + pieces]
-    masks = 2 if keyed else 1
-    mask_refs = refs[1 + pieces : 1 + pieces + masks]
-    weight_refs = refs[1 + pieces + masks : 3 + pieces + masks]
-    away_ref, keep_ref = refs[3 + pieces + masks :]
-    rows = q_ref.shape[0]
-    step = pl.program_id(0)
-    half = pl.num_programs(0) // 2
+    q_refs = refs[:2]
+    kv_refs = refs[2 : 2 + pieces]
+    mask_refs = refs[2 + pieces : 4 + pieces]
+    rest = refs[4 + pieces :]
     if keyed:
-        ids = mask_refs[0][...]
-        biases = [
-            jnp.where(ids == mask_refs[1][i], 0.0, NEGATIVE).astype(jnp.float32)
-            for i in range(pieces)
-        ]
-    else:
-        biases = [mask_refs[0][0, i] for i in range(pieces)]
+        key_ids, rest = rest[0], rest[1:]
+    weight_refs = rest[:2]
+    away_ref, keep_ref = rest[2:]
+    block = q_refs[0].shape[0]
+    rows = 2 * block
     lane = lax.broadcasted_iota(jnp.int32, (rows, LANES), 1)
+
+    def biased(scores, piece):
+        parts = []
+        for place in range(2):
+            part = scores[place * block : (place + 1) * block]
+            if keyed:
+                part = jnp.where(mask_refs[place][...] == key_ids[piece], part, NEGATIVE)
+            else:
+                part = part + mask_refs[place][0, piece]
+            parts.append(part)
+        return jnp.concatenate(parts, axis=0)
+
     mixed = []
     for pair in range(2):
-        queries = q_ref[:, pair * LANES : (pair + 1) * LANES]
+        cols = slice(pair * LANES, (pair + 1) * LANES)
+        queries = jnp.concatenate([q_refs[0][:, cols], q_refs[1][:, cols]], axis=0)
+        queries = queries.astype(jnp.float32) * HD ** (-0.5)
         key_cols = slice(2 * pair * LANES, (2 * pair + 1) * LANES)
         value_cols = slice((2 * pair + 1) * LANES, (2 * pair + 2) * LANES)
         merged = None
         for odd in range(LANES // HD):
             mine = (lane >= odd * HD) & (lane < (odd + 1) * HD)
-            picked = jnp.where(mine, queries.astype(jnp.float32) * HD ** (-0.5), 0.0).astype(
-                jnp.bfloat16
-            )
+            picked = jnp.where(mine, queries, 0.0).astype(jnp.bfloat16)
             scores = [
-                lax.dot_general(
-                    picked,
-                    kv_refs[i][:, key_cols],
-                    (((1,), (1,)), ((), ())),
-                    preferred_element_type=jnp.float32,
+                biased(
+                    lax.dot_general(
+                        picked,
+                        kv_refs[i][:, key_cols],
+                        (((1,), (1,)), ((), ())),
+                        preferred_element_type=jnp.float32,
+                    ),
+                    i,
                 )
-                + biases[i]
                 for i in range(pieces)
             ]
             top = functools.reduce(
@@ -466,44 +483,62 @@
                 total = part if total is None else total + part
             out_ref[:, cols] = total.astype(jnp.bfloat16)
 
-    @pl.when(step < half)
+    half = pl.num_programs(0) // 2
+
+    @pl.when(pl.program_id(0) < half)
     def _():
         write(away_ref)
 
-    @pl.when(step >= half)
+    @pl.when(pl.program_id(0) >= half)
     def _():
         write(keep_ref)
 
 
 def attend_pair(queries, kv_list, masks, keyed, weights, o_start, order):
     rows = queries.shape[0]
-    blocks = rows // BLOCK
+    steps = rows // (2 * BLOCK)
     features = weights[0].shape[0]
     pieces = len(kv_list)
     whole = lambda value: pl.BlockSpec(value.shape, lambda i, o: (0,) * value.ndim)
+    width = queries.shape[1]
+    q_specs = [
+        pl.BlockSpec((BLOCK, width), lambda i, o: (o[2 * i], 0)),
+        pl.BlockSpec((BLOCK, width), lambda i, o: (o[2 * i + 1], 0)),
+    ]
     if keyed:
-        mask_specs = [pl.BlockSpec((BLOCK, 1), lambda i, o: (o[i], 0)), whole(masks[1])]
+        mask_specs = [
+            pl.BlockSpec((BLOCK, 1), lambda i, o: (o[2 * i], 0)),
+            pl.BlockSpec((BLOCK, 1), lambda i, o: (o[2 * i + 1], 0)),
+            whole(masks[1]),
+        ]
+        masks = [masks[0], masks[0], masks[1]]
     else:
-        mask_specs = [pl.BlockSpec((1,) + masks[0].shape[1:], lambda i, o: (o[i], 0, 0, 0))]
-    half = blocks // 2
+        block = (1,) + masks[0].shape[1:]
+        mask_specs = [
+            pl.BlockSpec(block, lambda i, o: (o[2 * i], 0, 0, 0)),
+            pl.BlockSpec(block, lambda i, o: (o[2 * i + 1], 0, 0, 0)),
+        ]
+        masks = [masks[0], masks[0]]
+    half = steps // 2
     out = jax.ShapeDtypeStruct((rows // 2, features), jnp.bfloat16)
+    placed = (2 * BLOCK, features)
     return pl.pallas_call(
         functools.partial(pair_attention_kernel, pieces, keyed, o_start),
         grid_spec=pltpu.PrefetchScalarGridSpec(
             num_scalar_prefetch=1,
-            grid=(blocks,),
-            in_specs=[pl.BlockSpec((BLOCK, queries.shape[1]), lambda i, o: (o[i], 0))]
+            grid=(steps,),
+            in_specs=q_specs
             + [whole(kv) for kv in kv_list]
             + mask_specs
             + [whole(weight) for weight in weights],
             out_specs=[
-                pl.BlockSpec((BLOCK, features), lambda i, o: (jnp.minimum(i, half - 1), 0)),
-                pl.BlockSpec((BLOCK, features), lambda i, o: (jnp.maximum(i - half, 0), 0)),
+                pl.BlockSpec(placed, lambda i, o: (jnp.minimum(i, half - 1), 0)),
+                pl.BlockSpec(placed, lambda i, o: (jnp.maximum(i - half, 0), 0)),
             ],
         ),
         out_shape=[out, out],
         compiler_params=pltpu.CompilerParams(dimension_semantics=("arbitrary",)),
-    )(order, queries, *kv_list, *masks, *weights)
+    )(order, queries, queries, *kv_list, *masks, *weights)
 
 
 def down_kernel(bands, order_ref, own_hidden, other_hidden, own, other, away_ref, keep_ref):
@@ -549,13 +584,15 @@
 
 
 def sum_over_head(away, keep):
-    came = exchange(away, "head", 1)
-    total = keep.astype(jnp.float32) + came.astype(jnp.float32)
-    bit = 2
+    bit = 1
+    total, other = keep, away
     while bit < lax.axis_size("head"):
-        sent = total.astype(jnp.bfloat16)
-        total = sent.astype(jnp.float32) + exchange(sent, "head", bit).astype(jnp.float32)
+        came = exchange(other, "head", bit)
+        total = total.astype(jnp.float32) + came.astype(jnp.float32)
+        other = total.astype(jnp.bfloat16)
         bit *= 2
+        if bit < lax.axis_size("head"):
+            total = other
     return total
 
 
@@ -615,7 +652,6 @@
     half_blocks = mesh_blocks // 2
     turns = jnp.arange(mesh_blocks, dtype=jnp.int32)
     order = (turns + (1 - side) * half_blocks) % mesh_blocks
-    sides = jnp.stack([1 - side, side]).astype(jnp.int32)
     barrier = lax.optimization_barrier
     kv_cols, q_cols = (0, 2 * LANES), (2 * LANES, LANES)
     o_start = 3 * LANES
@@ -627,11 +663,6 @@
     enc_qo_other = [whole_pack(enc_in, enc_out, "qo", True)]
     for piece in enc_qo_own[1:]:
         enc_qo_other.append(swap(piece))
-    early = barrier((pack(proc_in, proc_out, "kvqo"), own_half(ff_up, 1), *enc_kv_pieces[1:]))
-    proc_own, up_own = [band_gather(value) for value in early[:2]]
-    proc_other = swap(proc_own)
-    up_other = swap(up_own)
-
     enc_bias = list_bias(enc_list, enc_count, band_index, mesh_blocks, grid_blocks)
     dec_bias = list_bias(dec_list, dec_count, band_index, grid_blocks, mesh_blocks)
     around, offsets, routes = slab_routes(bands, mesh_rows)
@@ -641,6 +672,20 @@
     mesh_norm = normed(mesh_feats)
 
     (enc_kv,) = project_placed(grid_norm, [enc_kv_pieces], 4 * LANES, False)
+    early = barrier(
+        (
+            pack(proc_in, proc_out, "kvqo"),
+            own_half(ff_up, 1),
+            own_half(ff_down, 0),
+            pack(dec_in, dec_out, "kvqo"),
+            enc_kv,
+        )
+    )
+    proc_own, up_own, down_own = [band_gather(value) for value in early[:3]]
+    dec_half = early[3]
+    proc_other = swap(proc_own)
+    up_other = swap(up_own)
+    down_other = swap(down_own)
     low, high = neighbours(enc_kv)
     enc_q, qo_own, qo_other = project_placed(
         mesh_norm, [enc_qo_own, enc_qo_other], LANES, True
@@ -650,30 +695,37 @@
     )
     state = half_of(mesh_feats, side).astype(jnp.float32) + sum_over_head(away, keep)
 
-    proc_norm = both_halves(normed(state), side)
-    proc_kv, proc_q = project_pair(proc_norm, proc_own, proc_other, [kv_cols, q_cols])
+    mine = normed(state)
+    theirs = exchange(mine, "head", 1)
+    proc_kv, proc_q = project_pair(
+        mine, theirs, side, proc_own, proc_other, [kv_cols, q_cols]
+    )
     slab = [proc_kv] + [lax.ppermute(proc_kv, "band", route) for route in routes]
-    late = barrier((own_half(ff_down, 0), pack(dec_in, dec_out, "kvqo"), *slab[1:]))
-    down_own = band_gather(late[0])
-    down_other = swap(down_own)
-    dec_own = band_gather(late[1])
+    dec_own = band_gather(barrier((dec_half, *slab[1:]))[0])
     dec_other = swap(dec_own)
     away, keep = attend_pair(
         proc_q, slab, [query_ids, key_ids], True, [proc_own, proc_other], o_start, order
     )
     state = state + sum_over_head(away, keep)
 
-    ff_norm = both_halves(normed(state), side)
-    hidden = [
-        jax.nn.gelu(dot(ff_norm, up), approximate=False).astype(jnp.bfloat16)
-        for up in (up_own, up_other)
-    ]
-    away, keep = down_pair(*hidden, down_own, down_other, sides)
+    mine = normed(state)
+    ff_norm = jnp.concatenate([exchange(mine, "head", 1), mine], axis=0)
+    hidden = [gelu(dot(ff_norm, up)).astype(jnp.bfloat16) for up in (up_own, up_other)]
+    away, keep = down_pair(*hidden, down_own, down_other, jnp.arange(2, dtype=jnp.int32))
     state = state + sum_over_head(away, keep)
 
-    final_norm = both_halves(normed(state), side)
-    (dec_q,) = project_pair(grid_norm, dec_own, dec_other, [q_cols])
-    (dec_kv,) = project_pair(final_norm, dec_own, dec_other, [kv_cols])
+    mine = normed(state)
+    theirs = exchange(mine, "head", 1)
+    (dec_kv,) = project_pair(mine, theirs, side, dec_own, dec_other, [kv_cols])
+    grid_half = grid_rows // 2
+    (dec_q,) = project_pair(
+        grid_norm[:grid_half],
+        grid_norm[grid_half:],
+        jnp.zeros((), jnp.int32),
+        dec_own,
+        dec_other,
+        [q_cols],
+    )
     low, high = neighbours(dec_kv)
     share = grid_rows // heads
     by_core = turns.reshape(-1, 2, share // BLOCK).transpose(1, 0, 2).reshape(2, -1)

time: 369 us -> 348 us (0.943)
  waiting for transfers between devices: 205 us -> 180 us
  starting transfers between devices: 45.6 us -> 55.8 us
  local copies, waits for them, and re-layouts: 12.5 us -> 18.5 us
  other arithmetic: 26.4 us -> 20.7 us
  matrix products: 10.6 us -> 5.93 us
    ppermute x3, waiting for transfers between devices: 57.7 us -> 41.1 us  [paired_device(): lax.ppermute(proc_kv, 'band', route)]
    ppermute x6, starting transfers between devices: 16.8 us -> 26.2 us  [from_bands(): lax.ppermute(value, 'band', [(i, (i - step) % bands) for i in range(bands)])]
    ppermute x6, waiting for transfers between devices: 11.7 us -> 4.36 us  [from_bands(): lax.ppermute(value, 'band', [(i, (i - step) % bands) for i in range(bands)])]
    dot_general x2, matrix products: 10.6 us -> 5.93 us  [dot(): return jnp.dot(a, b, preferred_element_type=jnp.float32)]
  transfers between devices with their start and end apart: 35 -> 35, of which waited for: 22 -> 22; matrix products, arithmetic and copies ran while one was open for 11% -> 10% of each run, Pallas kernels for 7% -> 9%
where the time goes in v2:
time: 348 us; the launch traced here: 346 us
  waiting for transfers between devices  180 us (52%)
  starting transfers between devices  55.8 us (16%)
  Pallas kernels  52.1 us (15%)
  other arithmetic  20.7 us (6%)
  local copies, waits for them, and re-layouts  18.5 us (5%)
  between operations  13.6 us (4%)
  matrix products  5.93 us (2%)
    ppermute x7, waiting for transfers between devices, swap(): return lax.ppermute(value, 'members', [(0, 1), (1, 0)])  52.6 us
    ppermute x11, waiting for transfers between devices, exchange(): return lax.ppermute(value, axis, [(i, i ^ bit) for i in range(count)])  50.8 us
    ppermute x3, waiting for transfers between devices, paired_device(): lax.ppermute(proc_kv, 'band', route)  41.1 us
    pallas_call x3, Pallas kernels, attend_pair(): pl.pallas_call(functools.partial(pair_attention_kernel, pieces, keyed, o_...  30.6 us
    ppermute x6, starting transfers between devices, from_bands(): lax.ppermute(value, 'band', [(i, (i - step) % bands) for i in range(bands)])  26.2 us
    all_gather x4, waiting for transfers between devices, band_gather(): return lax.all_gather(value, 'band', axis=0, tiled=True)  23.5 us
    pallas_call x3, Pallas kernels, project_pair(): pl.pallas_call(functools.partial(project_kernel, widths), in_specs=[pl.Bl...  10.5 us
    ppermute x7, starting transfers between devices, swap(): return lax.ppermute(value, 'members', [(0, 1), (1, 0)])  9.51 us
  transfers between devices with their start and end apart: 35, of which 22 were waited for; matrix products, arithmetic and copies ran while one was open for 10% of the time, Pallas kernels for 9%

profile of v2, /device:TPU:0, one launch (start us, length us, event | category | flops | bytes accessed | tf_op | source)
XLA Modules:
  0.0 346.4 jit_solution(17705774502962501073)
XLA Ops:
  9.0 5.1 %collective-permute-start.3 = (bf16[256,256]{1,0:T(8,128)(2,1)S(1)}, bf16[256,256]{1,0:T(8,128)(2,1)}, u32[]{:S(2)}, u32[]{:S(2)}) collective-permute-start(bf16[256,256]{1,0:T(8,128)(2,1)S(1)} %maximum_maximum_fusion.2.refs_1_), channel_id=1, source_target_pairs={{0,12},{4,0},{8,4},{12,8},{1,13},{5,1},{9,5},{13,9},{2,14},{6,2},{... | collective-permute-start | bytes 393224 | tf_op jit(solution)/shard_map/ppermute | solution.py:331
  27.5 16.1 %collective-permute-start.5 = (bf16[256,256]{1,0:T(8,128)(2,1)S(1)}, bf16[256,256]{1,0:T(8,128)(2,1)S(1)}, u32[]{:S(2)}, u32[]{:S(2)}) collective-permute-start(bf16[256,256]{1,0:T(8,128)(2,1)S(1)} %maximum_maximum_fusion.2.refs_1_), channel_id=1, source_target_pairs={{0,4},{4,8},{8,12},{12,0},{1,5},{5,9},{9,13},{13,1},{2,6},{6,10},{... | collective-permute-start | bytes 393224 | tf_op jit(solution)/shard_map/ppermute | solution.py:331
  43.6 4.3 %collective-permute-done.1.refs_3_ = bf16[256,512]{1,0:T(8,128)(2,1)} collective-permute-done((bf16[256,512]{1,0:T(8,128)(2,1)S(1)}, bf16[256,512]{1,0:T(8,128)(2,1)}, u32[]{:S(2)}, u32[]{:S(2)}) %collective-permute-start.1) | collective-permute-done | bytes 262176 | tf_op jit(solution)/shard_map/ppermute | solution.py:331
  52.5 4.6 %collective-permute-start.9 = (bf16[512,512]{1,0:T(8,128)(2,1)}, bf16[512,512]{1,0:T(8,128)(2,1)S(1)}, u32[]{:S(2)}, u32[]{:S(2)}) collective-permute-start(bf16[512,512]{1,0:T(8,128)(2,1)} %shard_map.145.refs_3_), channel_id=1, source_target_pairs={{0,4},{4,8},{8,12},{1,5},{5,9},{9,13},{2,6},{6,10},{10,14},{3,7},{... | collective-permute-start | bytes 1572872 | tf_op jit(solution)/shard_map/ppermute | solution.py:167
  76.5 9.4 %shard_map.147 = (bf16[256,1024]{1,0:T(8,128)(2,1)}, bf16[256,1024]{1,0:T(8,128)(2,1)}) custom-call(s32[4]{0:T(128)} %and_select_fusion.order_ref, bf16[512,256]{1,0:T(8,128)(2,1)} %get-tuple-element.24.refs_0_.refs_1_, bf16[512,256]{1,0:T(8,128)(2,1)} %get-tuple-element.24.refs_0_.refs_1_, bf16[512,512]{1,0:T(8,128)(2,1)} %copy-done.15, ...), custom_call_target="tpu_custom_call" | custom-call | tf_op jit(solution)/shard_map/pallas_call | solution.py:525
  89.8 12.5 %collective-permute-done.12 = bf16[256,1024]{1,0:T(8,128)(2,1)S(1)} collective-permute-done((bf16[256,1024]{1,0:T(8,128)(2,1)S(1)}, bf16[256,1024]{1,0:T(8,128)(2,1)S(1)}, u32[]{:S(2)}, u32[]{:S(2)}) %collective-permute-start.12) | collective-permute-done | bytes 524320 | tf_op jit(solution)/shard_map/ppermute | solution.py:37
  102.6 11.4 %all-gather.5.cloned.1.call-done.refs_2_.refs_9_ = bf16[1024,512]{1,0:T(8,128)(2,1)} async-done(((bf16[256,512]{1,0:T(8,128)(2,1)}), bf16[1024,512]{1,0:T(8,128)(2,1)}) %all-gather.5.cloned.1.call-update) | async-done | bytes 1048592 | tf_op jit(solution)/shard_map/all_gather | solution.py:390
  118.1 20.6 %collective-permute-done.14.refs_3_.refs_10_ = bf16[1024,512]{1,0:T(8,128)(2,1)} collective-permute-done((bf16[1024,512]{1,0:T(8,128)(2,1)}, bf16[1024,512]{1,0:T(8,128)(2,1)}, u32[]{:S(2)}, u32[]{:S(2)}) %collective-permute-start.14) | collective-permute-done | bytes 1048608 | tf_op jit(solution)/shard_map/ppermute | solution.py:373
  138.7 3.8 %shard_map.148 = (bf16[512,512]{1,0:T(8,128)(2,1)}, bf16[512,256]{1,0:T(8,128)(2,1)}) custom-call(s32[1]{0:T(128)} %bitcast.12.side_ref, bf16[256,1024]{1,0:T(8,128)(2,1)} %copy-done.6, bf16[256,1024]{1,0:T(8,128)(2,1)} %copy-done.16, bf16[1024,512]{1,0:T(8,128)(2,1)} %all-gather.5.cloned.1.call-done.refs_2_.refs_9_, ...), custom_call_target="tpu_custom_call" | custom-call | tf_op jit(solution)/shard_map/pallas_call | solution.py:408
  148.0 9.4 %collective-permute-done.15.refs_3_ = bf16[512,512]{1,0:T(8,128)(2,1)S(1)} collective-permute-done((bf16[512,512]{1,0:T(8,128)(2,1)}, bf16[512,512]{1,0:T(8,128)(2,1)S(1)}, u32[]{:S(2)}, u32[]{:S(2)}) %collective-permute-start.15) | collective-permute-done | bytes 524320 | tf_op jit(solution)/shard_map/ppermute | solution.py:703
  157.4 31.7 %collective-permute-done.16.refs_4_ = bf16[512,512]{1,0:T(8,128)(2,1)S(1)} collective-permute-done((bf16[512,512]{1,0:T(8,128)(2,1)}, bf16[512,512]{1,0:T(8,128)(2,1)S(1)}, u32[]{:S(2)}, u32[]{:S(2)}) %collective-permute-start.16) | collective-permute-done | bytes 524320 | tf_op jit(solution)/shard_map/ppermute | solution.py:703
  189.9 11.6 %shard_map.150 = (bf16[256,1024]{1,0:T(8,128)(2,1)}, bf16[256,1024]{1,0:T(8,128)(2,1)}) custom-call(s32[4]{0:T(128)} %and_select_fusion.order_ref, bf16[512,256]{1,0:T(8,128)(2,1)} %get-tuple-element.32.refs_0_.refs_1_, bf16[512,256]{1,0:T(8,128)(2,1)} %get-tuple-element.32.refs_0_.refs_1_, bf16[512,512]{1,0:T(8,128)(2,1)} %get-tuple-element.30.refs_2_, ...), custom_call_target="tpu_custom_call" | custom-call | tf_op jit(solution)/shard_map/pallas_call | solution.py:525
  208.0 11.0 %collective-permute-done.20 = bf16[256,1024]{1,0:T(8,128)(2,1)} collective-permute-done((bf16[256,1024]{1,0:T(8,128)(2,1)S(1)}, bf16[256,1024]{1,0:T(8,128)(2,1)}, u32[]{:S(2)}, u32[]{:S(2)}) %collective-permute-start.20) | collective-permute-done | bytes 524320 | tf_op jit(solution)/shard_map/ppermute | solution.py:37
  221.3 12.0 %all-gather.11.cloned.1.call-done.own = bf16[2048,256]{1,0:T(8,128)(2,1)} async-done(((bf16[512,256]{1,0:T(8,128)(2,1)}), bf16[2048,256]{1,0:T(8,128)(2,1)}) %all-gather.11.cloned.1.call-update) | async-done | bytes 1048592 | tf_op jit(solution)/shard_map/all_gather | solution.py:390
  240.8 17.2 %collective-permute-done.23.other = bf16[2048,256]{1,0:T(8,128)(2,1)S(1)} collective-permute-done((bf16[2048,256]{1,0:T(8,128)(2,1)}, bf16[2048,256]{1,0:T(8,128)(2,1)S(1)}, u32[]{:S(2)}, u32[]{:S(2)}) %collective-permute-start.23) | collective-permute-done | bytes 1048608 | tf_op jit(solution)/shard_map/ppermute | solution.py:373
  259.0 4.9 %shard_map.151 = (bf16[256,1024]{1,0:T(8,128)(2,1)}, bf16[256,1024]{1,0:T(8,128)(2,1)}) custom-call(s32[2]{0:T(128)} %iota.39.order_ref, bf16[512,512]{1,0:T(8,128)(2,1)} %multiply_convert_fusion.2.own_hidden, bf16[512,512]{1,0:T(8,128)(2,1)} %multiply_convert_fusion.1.other_hidden, bf16[2048,256]{1,0:T(8,128)(2,1)} %all-gather.11.cloned.1.call-done.own, ...), custom_call_target="tpu_custom_call" | custom-call | tf_op jit(solution)/shard_map/pallas_call | solution.py:573
  270.2 11.0 %collective-permute-done.25 = bf16[256,1024]{1,0:T(8,128)(2,1)S(1)} collective-permute-done((bf16[256,1024]{1,0:T(8,128)(2,1)S(1)}, bf16[256,1024]{1,0:T(8,128)(2,1)S(1)}, u32[]{:S(2)}, u32[]{:S(2)}) %collective-permute-start.25) | collective-permute-done | bytes 524320 | tf_op jit(solution)/shard_map/ppermute | solution.py:37
  282.9 11.1 %collective-permute-done.18.refs_3_.refs_8_ = bf16[1024,512]{1,0:T(8,128)(2,1)} collective-permute-done((bf16[1024,512]{1,0:T(8,128)(2,1)}, bf16[1024,512]{1,0:T(8,128)(2,1)}, u32[]{:S(2)}, u32[]{:S(2)}) %collective-permute-start.18) | collective-permute-done | bytes 1048608 | tf_op jit(solution)/shard_map/ppermute | solution.py:373
  294.8 3.4 shard_map.152.refs_3_
  305.3 3.3 shard_map.149.refs_0_.refs_1_
  308.6 3.2 collective-permute-done.27.refs_2_
  311.8 4.0 %collective-permute-done.28.refs_4_ = bf16[512,512]{1,0:T(8,128)(2,1)S(1)} collective-permute-done((bf16[512,512]{1,0:T(8,128)(2,1)}, bf16[512,512]{1,0:T(8,128)(2,1)S(1)}, u32[]{:S(2)}, u32[]{:S(2)}) %collective-permute-start.28) | collective-permute-done | bytes 524320 | tf_op jit(solution)/shard_map/ppermute | solution.py:167
  316.7 9.6 %shard_map.153 = (bf16[256,1024]{1,0:T(8,128)(2,1)}, bf16[256,1024]{1,0:T(8,128)(2,1)}) custom-call(s32[4]{0:T(128)} %broadcast_select_fusion.2.order_ref, bf16[512,256]{1,0:T(8,128)(2,1)} %shard_map.149.refs_0_.refs_1_, bf16[512,256]{1,0:T(8,128)(2,1)} %shard_map.149.refs_0_.refs_1_, bf16[512,512]{1,0:T(8,128)(2,1)} %copy-done.11, ...), custom_call_target="tpu_custom_call" | custom-call | tf_op jit(solution)/shard_map/pallas_call | solution.py:525
  330.3 7.8 %collective-permute-done.30 = bf16[1,128,1024]{2,1,0:T(8,128)(2,1)S(1)} collective-permute-done((bf16[1,128,1024]{2,1,0:T(8,128)(2,1)S(1)}, bf16[1,128,1024]{2,1,0:T(8,128)(2,1)S(1)}, u32[]{:S(2)}, u32[]{:S(2)}) %collective-permute-start.30) | collective-permute-done | bytes 262176 | tf_op jit(solution)/shard_map/ppermute | solution.py:37
  (208 shorter events, 93.7 us)
Async XLA Ops:
  6.5 107.5 %all-gather.5.cloned.1.call-start = ((), (), s32[]{:S(2)}) async-start(), calls=%async_computation | async-start | bytes 1310720 | tf_op jit(solution)/shard_map/all_gather | solution.py:390
  9.0 52.6 %collective-permute-start.3 = (bf16[256,256]{1,0:T(8,128)(2,1)S(1)}, bf16[256,256]{1,0:T(8,128)(2,1)}, u32[]{:S(2)}, u32[]{:S(2)}) collective-permute-start(bf16[256,256]{1,0:T(8,128)(2,1)S(1)} %maximum_maximum_fusion.2.refs_1_), channel_id=1, source_target_pairs={{0,12},{4,0},{8,4},{12,8},{1,13},{5,1},{9,5},{13,9},{2,14},{6,2},{... | collective-permute-start | bytes 393224 | tf_op jit(solution)/shard_map/ppermute | solution.py:331
  14.2 49.0 %collective-permute-start.4 = (bf16[256,256]{1,0:T(8,128)(2,1)S(1)}, bf16[256,256]{1,0:T(8,128)(2,1)}, u32[]{:S(2)}, u32[]{:S(2)}) collective-permute-start(bf16[256,256]{1,0:T(8,128)(2,1)S(1)} %maximum_maximum_fusion.2.refs_1_), channel_id=1, source_target_pairs={{0,8},{4,12},{8,0},{12,4},{1,9},{5,13},{9,1},{13,5},{2,10},{6,14},... | collective-permute-start | bytes 393224 | tf_op jit(solution)/shard_map/ppermute | solution.py:331
  14.7 33.2 %collective-permute-start.1 = (bf16[256,512]{1,0:T(8,128)(2,1)S(1)}, bf16[256,512]{1,0:T(8,128)(2,1)}, u32[]{:S(2)}, u32[]{:S(2)}) collective-permute-start(bf16[256,512]{1,0:T(8,128)(2,1)S(1)} %pad_maximum_fusion.7.refs_1_), channel_id=1, source_target_pairs={{0,8},{4,12},{8,0},{12,4},{1,9},{5,13},{9,1},{13,5},{2,10},{6,14},... | collective-permute-start | bytes 786440 | tf_op jit(solution)/shard_map/ppermute | solution.py:331
  17.3 30.7 %collective-permute-start.2 = (bf16[256,512]{1,0:T(8,128)(2,1)S(1)}, bf16[256,512]{1,0:T(8,128)(2,1)}, u32[]{:S(2)}, u32[]{:S(2)}) collective-permute-start(bf16[256,512]{1,0:T(8,128)(2,1)S(1)} %pad_maximum_fusion.7.refs_1_), channel_id=1, source_target_pairs={{0,4},{4,8},{8,12},{12,0},{1,5},{5,9},{9,13},{13,1},{2,6},{6,10},{... | collective-permute-start | bytes 786440 | tf_op jit(solution)/shard_map/ppermute | solution.py:331
  27.5 36.1 %collective-permute-start.5 = (bf16[256,256]{1,0:T(8,128)(2,1)S(1)}, bf16[256,256]{1,0:T(8,128)(2,1)S(1)}, u32[]{:S(2)}, u32[]{:S(2)}) collective-permute-start(bf16[256,256]{1,0:T(8,128)(2,1)S(1)} %maximum_maximum_fusion.2.refs_1_), channel_id=1, source_target_pairs={{0,4},{4,8},{8,12},{12,0},{1,5},{5,9},{9,13},{13,1},{2,6},{6,10},{... | collective-permute-start | bytes 393224 | tf_op jit(solution)/shard_map/ppermute | solution.py:331
  51.0 24.4 %collective-permute-start.10 = (bf16[512,512]{1,0:T(8,128)(2,1)}, bf16[512,512]{1,0:T(8,128)(2,1)S(1)}, u32[]{:S(2)}, u32[]{:S(2)}) collective-permute-start(bf16[512,512]{1,0:T(8,128)(2,1)} %shard_map.145.refs_3_), channel_id=1, source_target_pairs={{4,0},{8,4},{12,8},{5,1},{9,5},{13,9},{6,2},{10,6},{14,10},{7,3},{... | collective-permute-start | bytes 1572872 | tf_op jit(solution)/shard_map/ppermute | solution.py:167
  52.5 23.0 %collective-permute-start.9 = (bf16[512,512]{1,0:T(8,128)(2,1)}, bf16[512,512]{1,0:T(8,128)(2,1)S(1)}, u32[]{:S(2)}, u32[]{:S(2)}) collective-permute-start(bf16[512,512]{1,0:T(8,128)(2,1)} %shard_map.145.refs_3_), channel_id=1, source_target_pairs={{0,4},{4,8},{8,12},{1,5},{5,9},{9,13},{2,6},{6,10},{10,14},{3,7},{... | collective-permute-start | bytes 1572872 | tf_op jit(solution)/shard_map/ppermute | solution.py:167
  87.6 118.9 %all-gather.9.cloned.1.call-start = ((), (), s32[]{:S(2)}) async-start(), calls=%async_computation.2 | async-start | bytes 1310720 | tf_op jit(solution)/shard_map/all_gather | solution.py:390
  88.3 14.0 %collective-permute-start.12 = (bf16[256,1024]{1,0:T(8,128)(2,1)S(1)}, bf16[256,1024]{1,0:T(8,128)(2,1)S(1)}, u32[]{:S(2)}, u32[]{:S(2)}) collective-permute-start(bf16[256,1024]{1,0:T(8,128)(2,1)S(1)} %add_convert_fusion.2), channel_id=1, source_target_pairs={{0,2},{1,3},{2,0},{3,1},{4,6},{5,7},{6,4},{7,5},{8,10},{9,11},{10,... | collective-permute-start | bytes 1572872 | tf_op jit(solution)/shard_map/ppermute | solution.py:37
  114.0 24.7 %collective-permute-start.14 = (bf16[1024,512]{1,0:T(8,128)(2,1)}, bf16[1024,512]{1,0:T(8,128)(2,1)}, u32[]{:S(2)}, u32[]{:S(2)}) collective-permute-start(bf16[1024,512]{1,0:T(8,128)(2,1)} %all-gather.5.cloned.1.call-done.refs_2_.refs_9_), channel_id=1, source_target_pairs={{0,16},{16,0},{1,17},{17,1},{2,18},{18,2},{3,19},{19,3},{4,20},{20... | collective-permute-start | bytes 3145736 | tf_op jit(solution)/shard_map/ppermute | solution.py:373
  116.2 117.1 %all-gather.11.cloned.1.call-start = ((), (), s32[]{:S(2)}) async-start(), calls=%async_computation.3 | async-start | bytes 1310720 | tf_op jit(solution)/shard_map/all_gather | solution.py:390
  142.6 14.8 %collective-permute-start.15 = (bf16[512,512]{1,0:T(8,128)(2,1)}, bf16[512,512]{1,0:T(8,128)(2,1)S(1)}, u32[]{:S(2)}, u32[]{:S(2)}) collective-permute-start(bf16[512,512]{1,0:T(8,128)(2,1)} %get-tuple-element.30.refs_2_), channel_id=1, source_target_pairs={{0,12},{4,0},{8,4},{12,8},{1,13},{5,1},{9,5},{13,9},{2,14},{6,2},{... | collective-permute-start | bytes 1572872 | tf_op jit(solution)/shard_map/ppermute | solution.py:703
  144.7 44.4 %collective-permute-start.16 = (bf16[512,512]{1,0:T(8,128)(2,1)}, bf16[512,512]{1,0:T(8,128)(2,1)S(1)}, u32[]{:S(2)}, u32[]{:S(2)}) collective-permute-start(bf16[512,512]{1,0:T(8,128)(2,1)} %get-tuple-element.30.refs_2_), channel_id=1, source_target_pairs={{0,8},{4,12},{8,0},{12,4},{1,9},{5,13},{9,1},{13,5},{2,10},{6,14},... | collective-permute-start | bytes 1572872 | tf_op jit(solution)/shard_map/ppermute | solution.py:703
  145.2 43.9 %collective-permute-start.17 = (bf16[512,512]{1,0:T(8,128)(2,1)}, bf16[512,512]{1,0:T(8,128)(2,1)}, u32[]{:S(2)}, u32[]{:S(2)}) collective-permute-start(bf16[512,512]{1,0:T(8,128)(2,1)} %get-tuple-element.30.refs_2_), channel_id=1, source_target_pairs={{0,4},{4,8},{8,12},{12,0},{1,5},{5,9},{9,13},{13,1},{2,6},{6,10},{... | collective-permute-start | bytes 1572872 | tf_op jit(solution)/shard_map/ppermute | solution.py:703
  204.9 14.1 %collective-permute-start.20 = (bf16[256,1024]{1,0:T(8,128)(2,1)S(1)}, bf16[256,1024]{1,0:T(8,128)(2,1)}, u32[]{:S(2)}, u32[]{:S(2)}) collective-permute-start(bf16[256,1024]{1,0:T(8,128)(2,1)S(1)} %add_convert_fusion.1), channel_id=1, source_target_pairs={{0,2},{1,3},{2,0},{3,1},{4,6},{5,7},{6,4},{7,5},{8,10},{9,11},{10,... | collective-permute-start | bytes 1572872 | tf_op jit(solution)/shard_map/ppermute | solution.py:37
  206.4 62.3 %all-gather.7.cloned.1.call-start = ((), (), s32[]{:S(2)}) async-start(), calls=%async_computation.1 | async-start | bytes 1310720 | tf_op jit(solution)/shard_map/all_gather | solution.py:390
  206.5 31.3 %collective-permute-start.22 = (bf16[1024,512]{1,0:T(8,128)(2,1)}, bf16[1024,512]{1,0:T(8,128)(2,1)}, u32[]{:S(2)}, u32[]{:S(2)}) collective-permute-start(bf16[1024,512]{1,0:T(8,128)(2,1)} %all-gather.9.cloned.1.call-done), channel_id=1, source_target_pairs={{0,16},{16,0},{1,17},{17,1},{2,18},{18,2},{3,19},{19,3},{4,20},{20... | collective-permute-start | bytes 3145736 | tf_op jit(solution)/shard_map/ppermute | solution.py:373
  221.2 13.6 %collective-permute-start.21 = (bf16[256,1024]{1,0:T(8,128)(2,1)S(1)}, bf16[256,1024]{1,0:T(8,128)(2,1)}, u32[]{:S(2)}, u32[]{:S(2)}) collective-permute-start(bf16[256,1024]{1,0:T(8,128)(2,1)S(1)} %multiply_convert_fusion.3), channel_id=1, source_target_pairs={{0,1},{1,0},{2,3},{3,2},{4,5},{5,4},{6,7},{7,6},{8,9},{9,8},{10,11... | collective-permute-start | bytes 1572872 | tf_op jit(solution)/shard_map/ppermute | solution.py:37
  233.3 24.6 %collective-permute-start.23 = (bf16[2048,256]{1,0:T(8,128)(2,1)}, bf16[2048,256]{1,0:T(8,128)(2,1)S(1)}, u32[]{:S(2)}, u32[]{:S(2)}) collective-permute-start(bf16[2048,256]{1,0:T(8,128)(2,1)} %all-gather.11.cloned.1.call-done.own), channel_id=1, source_target_pairs={{0,16},{16,0},{1,17},{17,1},{2,18},{18,2},{3,19},{19,3},{4,20},{20... | collective-permute-start | bytes 3145736 | tf_op jit(solution)/shard_map/ppermute | solution.py:373
  267.2 14.0 %collective-permute-start.25 = (bf16[256,1024]{1,0:T(8,128)(2,1)S(1)}, bf16[256,1024]{1,0:T(8,128)(2,1)S(1)}, u32[]{:S(2)}, u32[]{:S(2)}) collective-permute-start(bf16[256,1024]{1,0:T(8,128)(2,1)S(1)} %add_convert_fusion), channel_id=1, source_target_pairs={{0,2},{1,3},{2,0},{3,1},{4,6},{5,7},{6,4},{7,5},{8,10},{9,11},{10,... | collective-permute-start | bytes 1572872 | tf_op jit(solution)/shard_map/ppermute | solution.py:37
  268.7 25.2 %collective-permute-start.18 = (bf16[1024,512]{1,0:T(8,128)(2,1)}, bf16[1024,512]{1,0:T(8,128)(2,1)}, u32[]{:S(2)}, u32[]{:S(2)}) collective-permute-start(bf16[1024,512]{1,0:T(8,128)(2,1)} %all-gather.7.cloned.1.call-done.refs_2_.refs_7_), channel_id=1, source_target_pairs={{0,16},{16,0},{1,17},{17,1},{2,18},{18,2},{3,19},{19,3},{4,20},{20... | collective-permute-start | bytes 3145736 | tf_op jit(solution)/shard_map/ppermute | solution.py:373
  298.1 13.7 %collective-permute-start.27 = (bf16[512,512]{1,0:T(8,128)(2,1)}, bf16[512,512]{1,0:T(8,128)(2,1)S(1)}, u32[]{:S(2)}, u32[]{:S(2)}) collective-permute-start(bf16[512,512]{1,0:T(8,128)(2,1)} %shard_map.152.refs_3_), channel_id=1, source_target_pairs={{0,4},{4,8},{8,12},{1,5},{5,9},{9,13},{2,6},{6,10},{10,14},{3,7},{... | collective-permute-start | bytes 1572872 | tf_op jit(solution)/shard_map/ppermute | solution.py:167
  301.2 14.6 %collective-permute-start.28 = (bf16[512,512]{1,0:T(8,128)(2,1)}, bf16[512,512]{1,0:T(8,128)(2,1)S(1)}, u32[]{:S(2)}, u32[]{:S(2)}) collective-permute-start(bf16[512,512]{1,0:T(8,128)(2,1)} %shard_map.152.refs_3_), channel_id=1, source_target_pairs={{4,0},{8,4},{12,8},{5,1},{9,5},{13,9},{6,2},{10,6},{14,10},{7,3},{... | collective-permute-start | bytes 1572872 | tf_op jit(solution)/shard_map/ppermute | solution.py:167
  (47 other events, 371.9 us)
Sparse Core Ops, SparseCore 0:
  87.7 26.2 all-gather.4
  116.4 26.5 all-gather.8
  206.5 26.7 all-gather.10
  235.0 27.2 all-gather.6
